TPU v7x, 32 devices: a whole 2x2x4 slice. The times are simulated.
32 devices in a mesh: dp: 2 (over x), tp: 4 (over z), cp: 4 (over y, core).
Axes of the slice: x: 2, y: 2, z: 4, core: 2. Of those that a mesh axis runs over, the one named last changes fastest.
Arguments:
- tokens_in: bfloat16 [12288, 3584], P(('dp', 'cp', 'tp')), parts along dimension 0
- grad_out: bfloat16 [12288, 3584], P(('dp', 'cp', 'tp')), parts along dimension 0
- w_query: bfloat16 [3584, 3584], P(None, 'tp')
- w_key: bfloat16 [3584, 512], P(None, 'tp')
- w_value: bfloat16 [3584, 512], P(None, 'tp')
- w_out: bfloat16 [3584, 3584], P('tp')
Outputs:
- output 1: bfloat16 [12288, 3584], P(('dp', 'cp', 'tp')), parts along dimension 0
- output 2: bfloat16 [12288, 3584], P(('dp', 'cp', 'tp')), parts along dimension 0
There are 2 independent parts. A program takes and returns all parts, laid end to end along the dimension named above; an argument that names none is the same for every part.
All inputs are finite; a program needn't handle non-finite values.
Results may differ from a plain program's by a relative error of at most 0.00951519.
Values are sent between devices in bfloat16 or wider.
A program may use at most 1 GiB of HBM per device.

v0:
```python
import jax
import jax.numpy as jnp
from jax import lax
from jax.sharding import PartitionSpec as P

HEAD_DIM = 128


def block_rows(piece_rows, key_rows, head_count):
    budget = max(1, (1 << 22) // (key_rows * head_count))
    row_count = 8
    for candidate in (16, 32, 64, 128):
        if candidate <= budget and piece_rows % candidate == 0:
            row_count = candidate
    return row_count


def fold_positions(row_ids, seq_loc, cp_size):
    piece_rows = seq_loc // 2
    shard_idx = row_ids // seq_loc
    within = row_ids % seq_loc
    piece_id = jnp.where(within < piece_rows, shard_idx, 2 * cp_size - 1 - shard_idx)
    return piece_id * piece_rows + within % piece_rows


def dot_transposed(left, right):
    return lax.dot_general(left, right, (((1,), (1,)), ((), ())), preferred_element_type=jnp.float32)


def solution(mesh):
    cp_size = mesh.shape['cp']
    row_spec = P(('dp', 'cp', 'tp'), None)

    def local_step(x_blk, dy_blk, w_query, w_key, w_value, w_out):
        cp_rank = lax.axis_index('cp')
        x_loc = lax.all_gather(x_blk, 'tp', axis=0, tiled=True)
        seq_loc = x_loc.shape[0]
        seq_all = seq_loc * cp_size
        piece_rows = seq_loc // 2
        heads_q = w_query.shape[1] // HEAD_DIM
        heads_kv = w_key.shape[1] // HEAD_DIM
        group_size = heads_q // heads_kv
        score_scale = HEAD_DIM ** -0.5
        query_loc = jnp.dot(x_loc, w_query, preferred_element_type=jnp.float32).astype(jnp.bfloat16).reshape(seq_loc, heads_kv, group_size, HEAD_DIM)
        keys_loc = jnp.dot(x_loc, w_key, preferred_element_type=jnp.float32).astype(jnp.bfloat16).reshape(seq_loc, heads_kv, HEAD_DIM)
        values_loc = jnp.dot(x_loc, w_value, preferred_element_type=jnp.float32).astype(jnp.bfloat16).reshape(seq_loc, heads_kv, HEAD_DIM)
        keys_all = lax.all_gather(keys_loc, 'cp', axis=0, tiled=True)
        values_all = lax.all_gather(values_loc, 'cp', axis=0, tiled=True)
        dy_loc = lax.all_gather(dy_blk, 'tp', axis=0, tiled=True)
        d_out = dot_transposed(dy_loc, w_out).astype(jnp.bfloat16).reshape(seq_loc, heads_kv, group_size, HEAD_DIM)
        key_pos = fold_positions(jnp.arange(seq_all, dtype=jnp.int32), seq_loc, cp_size)
        query_pos = fold_positions(cp_rank * seq_loc + jnp.arange(seq_loc, dtype=jnp.int32), seq_loc, cp_size)
        blk_rows = block_rows(piece_rows, seq_all, heads_q)
        block_count = seq_loc // blk_rows

        def block_step(acc_pair, blk_in):
            dk_acc, dv_acc = acc_pair
            q_blk, do_blk, pos_blk = blk_in
            scores = jnp.einsum('qhgd,khd->hgqk', q_blk, keys_all, preferred_element_type=jnp.float32) * score_scale
            allowed = pos_blk[:, None] >= key_pos[None, :]
            scores = jnp.where(allowed, scores, -jnp.inf)
            log_norm = jax.nn.logsumexp(scores, axis=-1, keepdims=True)
            prob_bf = jnp.exp(scores - log_norm).astype(jnp.bfloat16)
            out_blk = jnp.einsum('hgqk,khd->qhgd', prob_bf, values_all, preferred_element_type=jnp.float32).astype(jnp.bfloat16)
            row_delta = jnp.einsum('qhgd,qhgd->hgq', do_blk, out_blk, preferred_element_type=jnp.float32)
            d_prob = jnp.einsum('qhgd,khd->hgqk', do_blk, values_all, preferred_element_type=jnp.float32)
            d_score = (prob_bf.astype(jnp.float32) * (d_prob - row_delta[..., None])).astype(jnp.bfloat16)
            dq_blk = (jnp.einsum('hgqk,khd->qhgd', d_score, keys_all, preferred_element_type=jnp.float32) * score_scale).astype(jnp.bfloat16)
            dk_acc = dk_acc + jnp.einsum('hgqk,qhgd->khd', d_score, q_blk, preferred_element_type=jnp.float32) * score_scale
            dv_acc = dv_acc + jnp.einsum('hgqk,qhgd->khd', prob_bf, do_blk, preferred_element_type=jnp.float32)
            return (dk_acc, dv_acc), (out_blk, dq_blk)

        zeros_kv = jnp.zeros((seq_all, heads_kv, HEAD_DIM), jnp.float32)
        blk_inputs = (query_loc.reshape(block_count, blk_rows, heads_kv, group_size, HEAD_DIM), d_out.reshape(block_count, blk_rows, heads_kv, group_size, HEAD_DIM), query_pos.reshape(block_count, blk_rows))
        (dk_part, dv_part), (out_blocks, dq_blocks) = lax.scan(block_step, (zeros_kv, zeros_kv), blk_inputs)
        attn_out = out_blocks.reshape(seq_loc, heads_q * HEAD_DIM)
        d_query = dq_blocks.reshape(seq_loc, heads_q * HEAD_DIM)
        y_part = jnp.dot(attn_out, w_out, preferred_element_type=jnp.float32)
        y_blk = lax.psum_scatter(y_part, 'tp', scatter_dimension=0, tiled=True).astype(jnp.bfloat16)
        dk_own = lax.psum_scatter(dk_part, 'cp', scatter_dimension=0, tiled=True).astype(jnp.bfloat16).reshape(seq_loc, heads_kv * HEAD_DIM)
        dv_own = lax.psum_scatter(dv_part, 'cp', scatter_dimension=0, tiled=True).astype(jnp.bfloat16).reshape(seq_loc, heads_kv * HEAD_DIM)
        dx_part = dot_transposed(d_query, w_query) + dot_transposed(dk_own, w_key) + dot_transposed(dv_own, w_value)
        dx_blk = lax.psum_scatter(dx_part, 'tp', scatter_dimension=0, tiled=True).astype(jnp.bfloat16)
        return y_blk, dx_blk

    return jax.shard_map(local_step, mesh=mesh, in_specs=(row_spec, row_spec, P(None, 'tp'), P(None, 'tp'), P(None, 'tp'), P('tp', None)), out_specs=(row_spec, row_spec), check_vma=False)
```

profile of v0, /device:TPU:0, one launch (start us, length us, event | category | flops | bytes accessed | tf_op | source)
XLA Modules:
  0.0 1980.8 jit_solution(6378152710793578181)
XLA Ops:
  8.8 196.3 %all-gather.7.cloned.1.call-done = bf16[1536,3584]{1,0:T(8,128)(2,1)} async-done(((bf16[384,3584]{1,0:T(8,128)(2,1)}), bf16[1536,3584]{1,0:T(8,128)(2,1)}) %all-gather.7.cloned.1.call-update) | async-done | bytes 11010064 | tf_op jit(solution)/shard_map/all_gather | solution.py:36
  205.1 6.6 convolution_convert_fusion.2
  211.8 186.0 %all-gather.9.cloned.1.call-done = bf16[1536,3584]{1,0:T(8,128)(2,1)} async-done(((bf16[384,3584]{1,0:T(8,128)(2,1)}), bf16[1536,3584]{1,0:T(8,128)(2,1)}) %all-gather.9.cloned.1.call-update) | async-done | bytes 11010064 | tf_op jit(solution)/shard_map/all_gather | solution.py:49
  397.7 16.8 convolution_convert_fusion
  414.6 6.3 reshape_reshape.7
  425.0 6.6 convolution_convert_fusion.3
  431.7 16.8 convolution_convert_fusion.1
  448.5 6.3 reshape_reshape.6
  459.1 702.0 %while.17 = (s32[]{:T(128)}, f32[6144,1,128]{0,2,1:T(8,128)}, f32[6144,1,128]{0,2,1:T(8,128)}, bf16[24,64,1,7,128]{4,1,3,2,0:T(8,128)(2,1)}, bf16[24,64,1,7,128]...) while((s32[]{:T(128)}, f32[6144,1,128]{0,2,1:T(8,128)}, ...), condition=%wide.region_3.4_spmd.clone, body=%wide.region_0.3_spmd.clone.sunk | while | flops 4263005440 | bytes 152097072 | solution.py:75
  469.0 4.8 fusion.125
  497.2 4.8 fusion.125
  502.7 4.8 fusion.128
  526.5 4.8 fusion.125
  532.0 4.8 fusion.128
  555.8 4.8 fusion.125
  561.3 4.8 fusion.128
  585.1 4.8 fusion.125
  590.6 4.8 fusion.128
  614.3 4.8 fusion.125
  619.9 4.8 fusion.128
  643.6 4.8 fusion.125
  649.1 4.8 fusion.128
  672.9 4.8 fusion.125
  678.4 4.8 fusion.128
  702.2 4.8 fusion.125
  707.7 4.8 fusion.128
  731.5 4.8 fusion.125
  737.0 4.8 fusion.128
  760.7 4.8 fusion.125
  766.3 4.8 fusion.128
  790.0 4.8 fusion.125
  795.5 4.8 fusion.128
  819.3 4.8 fusion.125
  824.8 4.8 fusion.128
  848.6 4.8 fusion.125
  854.1 4.8 fusion.128
  877.9 4.8 fusion.125
  883.4 4.8 fusion.128
  907.1 4.8 fusion.125
  912.7 4.8 fusion.128
  936.4 4.8 fusion.125
  941.9 4.8 fusion.128
  965.7 4.8 fusion.125
  971.2 4.8 fusion.128
  995.0 4.8 fusion.125
  1000.5 4.8 fusion.128
  1024.3 4.8 fusion.125
  1029.8 4.8 fusion.128
  1053.5 4.8 fusion.125
  1059.1 4.8 fusion.128
  1082.8 4.8 fusion.125
  1088.3 4.8 fusion.128
  1112.1 4.8 fusion.125
  1117.6 4.8 fusion.128
  1141.4 4.8 fusion.125
  1146.9 4.8 fusion.128
  1166.0 17.9 fusion.65
  1188.2 18.2 fusion.62
  1206.4 10.5 fusion.69
  1216.9 20.0 %reduce-scatter.9.cloned.1.call-done = f32[1536,1,128]{0,2,1:T(8,128)} async-done(((f32[6144,1,128]{0,2,1:T(8,128)}), f32[1536,1,128]{0,2,1:T(8,128)}) %reduce-scatter.9.cloned.1.call-update) | async-done | bytes 786448 | tf_op jit(solution)/shard_map/reduce_scatter | solution.py:81
  1236.9 23.4 %add_add_fusion = f32[1536,3584]{1,0:T(8,128)} fusion(f32[1536,3584]{1,0:T(8,128)} %fusion.62, f32[1536,3584]{1,0:T(8,128)} %fusion.69, bf16[3584,128]{1,0:T(8,128)(2,1)S(1)} %copy-done.7, f32[1536,1,128]{0,2,1:T(8,128)} %reduce-scatter.9.cloned.1.call-done), kind=kOutput, calls=%fused_computation.67 | convolution fusion | flops 1420492800 | bytes 67764224 | tf_op jit(solution)/shard_map/dot_general | solution.py:27
  1260.4 342.2 %reduce-scatter.5.cloned.1.call-done = f32[384,3584]{1,0:T(8,128)} async-done(((f32[1536,3584]{1,0:T(8,128)}), f32[384,3584]{1,0:T(8,128)}) %reduce-scatter.5.cloned.1.call-update) | async-done | bytes 5505040 | tf_op jit(solution)/shard_map/reduce_scatter | solution.py:79
  1602.5 4.4 convert_element_type.61
  1606.9 362.2 %reduce-scatter.11.cloned.1.call-done = f32[384,3584]{1,0:T(8,128)} async-done(((f32[1536,3584]{1,0:T(8,128)}), f32[384,3584]{1,0:T(8,128)}) %reduce-scatter.11.cloned.1.call-update) | async-done | bytes 5505040 | tf_op jit(solution)/shard_map/reduce_scatter | solution.py:83
  (564 shorter events, 495.9 us)
Async XLA Ops:
  7.2 417.9 %copy-start = (bf16[3584,128]{1,0:T(8,128)(2,1)S(1)}, bf16[3584,128]{1,0:T(8,128)(2,1)}, u32[]{:S(2)}) copy-start(bf16[3584,128]{1,0:T(8,128)(2,1)} %param.11) | copy-start | bytes 2752516
  7.2 197.9 %copy-start.6 = (bf16[3584,128]{1,0:T(8,128)(2,1)S(1)}, bf16[3584,128]{1,0:T(8,128)(2,1)}, u32[]{:S(2)}) copy-start(bf16[3584,128]{1,0:T(8,128)(2,1)} %param.12) | copy-start | bytes 2752516
  7.2 197.9 %all-gather.7.cloned.1.call-start = ((), (), s32[]{:S(2)}) async-start(), calls=%async_computation.4 | async-start | bytes 13762560 | tf_op jit(solution)/shard_map/all_gather | solution.py:36
  7.9 389.8 %all-gather.9.cloned.1.call-start = ((), (), s32[]{:S(2)}) async-start(), calls=%async_computation.5 | async-start | bytes 13762560 | tf_op jit(solution)/shard_map/all_gather | solution.py:49
  8.7 450.4 %all-gather.13.cloned.1.call-start = ((), (), s32[]{:S(2)}) async-start(), calls=%async_computation.11 | async-start | bytes 1966080 | tf_op jit(solution)/shard_map/all_gather | solution.py:48
  211.7 247.3 %all-gather.11.cloned.1.call-start = ((), (), s32[]{:S(2)}) async-start(), calls=%async_computation.10 | async-start | bytes 1966080 | tf_op jit(solution)/shard_map/all_gather | solution.py:47
  431.6 774.8 %reduce-scatter.7.cloned.1.call-start = ((), (), s32[]{:S(2)}) async-start(), calls=%async_computation.7 | async-start | bytes 3932160 | tf_op jit(solution)/shard_map/reduce_scatter | solution.py:80
  469.0 5.5 copy-start.1
  474.5 3.8 copy-start.4
  478.3 2.6 copy-start.5
  497.2 5.5 copy-start.1
  502.7 4.8 copy-start.4
  507.6 2.6 copy-start.5
  526.5 5.5 copy-start.1
  532.0 4.8 copy-start.4
  536.9 2.6 copy-start.5
  555.8 5.5 copy-start.1
  561.3 4.8 copy-start.4
  566.1 2.6 copy-start.5
  585.1 5.5 copy-start.1
  590.6 4.8 copy-start.4
  595.4 2.6 copy-start.5
  614.3 5.5 copy-start.1
  619.9 4.8 copy-start.4
  643.6 5.5 copy-start.1
  649.1 4.8 copy-start.4
  672.9 5.5 copy-start.1
  678.4 4.8 copy-start.4
  702.2 5.5 copy-start.1
  707.7 4.8 copy-start.4
  731.5 5.5 copy-start.1
  737.0 4.8 copy-start.4
  760.7 5.5 copy-start.1
  766.3 4.8 copy-start.4
  790.0 5.5 copy-start.1
  795.5 4.8 copy-start.4
  819.3 5.5 copy-start.1
  824.8 4.8 copy-start.4
  848.6 5.5 copy-start.1
  854.1 4.8 copy-start.4
  877.9 5.5 copy-start.1
  883.4 4.8 copy-start.4
  907.1 5.5 copy-start.1
  912.7 4.8 copy-start.4
  936.4 5.5 copy-start.1
  941.9 4.8 copy-start.4
  965.7 5.5 copy-start.1
  971.2 4.8 copy-start.4
  995.0 5.5 copy-start.1
  1000.5 4.8 copy-start.4
  1024.3 5.5 copy-start.1
  1029.8 4.8 copy-start.4
  1053.5 5.5 copy-start.1
  1059.1 4.8 copy-start.4
  1082.8 5.5 copy-start.1
  1088.3 4.8 copy-start.4
  1112.1 5.5 copy-start.1
  1117.6 4.8 copy-start.4
  1141.4 5.5 copy-start.1
  1146.9 4.8 copy-start.4
  1161.1 75.8 %reduce-scatter.9.cloned.1.call-start = ((), (), s32[]{:S(2)}) async-start(), calls=%async_computation.8 | async-start | bytes 3932160 | tf_op jit(solution)/shard_map/reduce_scatter | solution.py:81
  1161.7 440.8 %reduce-scatter.5.cloned.1.call-start = ((), (), s32[]{:S(2)}) async-start(), calls=%async_computation.6 | async-start | bytes 27525120 | tf_op jit(solution)/shard_map/reduce_scatter | solution.py:79
  1183.9 785.1 %reduce-scatter.11.cloned.1.call-start = ((), (), s32[]{:S(2)}) async-start(), calls=%async_computation.9 | async-start | bytes 27525120 | tf_op jit(solution)/shard_map/reduce_scatter | solution.py:83
  1206.4 30.5 %copy-start.7 = (bf16[3584,128]{1,0:T(8,128)(2,1)S(1)}, bf16[3584,128]{1,0:T(8,128)(2,1)}, u32[]{:S(2)}) copy-start(bf16[3584,128]{1,0:T(8,128)(2,1)} %param.12) | copy-start | bytes 2752516
  (67 other events, 144.1 us)
Sparse Core Ops, SparseCore 0:
  9.6 195.4 all-gather.6
  206.7 191.0 all-gather.8
  399.3 17.6 all-gather.12
  431.8 17.6 all-gather.10
  1161.2 35.7 reduce-scatter.6
  1199.4 37.4 reduce-scatter.8
  1239.3 363.1 reduce-scatter.4
  1604.9 364.1 reduce-scatter.10
where the time goes:
time: 1990 us; the launch traced here: 1980 us
  waiting for transfers between devices  1110 us (56%)
  matrix products  611 us (31%)
  other arithmetic  158 us (8%)
  local copies, waits for them, and re-layouts  85.5 us (4%)
    reduce_scatter x1, waiting for transfers between devices, local_step(): lax.psum_scatter(dx_part, 'tp', scatter_dimension=0, tiled=True)  362 us
    reduce_scatter x1, waiting for transfers between devices, local_step(): lax.psum_scatter(y_part, 'tp', scatter_dimension=0, tiled=True)  342 us
    all_gather x1, waiting for transfers between devices, local_step(): x_loc = lax.all_gather(x_blk, 'tp', axis=0, tiled=True)  196 us
    all_gather x1, waiting for transfers between devices, local_step(): dy_loc = lax.all_gather(dy_blk, 'tp', axis=0, tiled=True)  186 us
    dot_general x24, matrix products, block_step(): jnp.einsum('hgqk,khd->qhgd', prob_bf, values_all, preferred_element_type=...  116 us
    dot_general x24, matrix products, block_step(): jnp.einsum('hgqk,qhgd->khd', prob_bf, do_blk, preferred_element_type=jnp....  115 us
    convert_element_type x24, other arithmetic, block_step(): prob_bf = jnp.exp(scores - log_norm).astype(jnp.bfloat16)  103 us
    dot_general x24, matrix products, block_step(): jnp.einsum('qhgd,khd->hgqk', q_blk, keys_all, preferred_element_type=jnp....  83.8 us
  transfers between devices with their start and end apart: 8, of which 5 were waited for; matrix products, arithmetic and copies ran while one was open for 8% of the time, Pallas kernels for 0%

commit v1 on v0

v1 whole, which is shorter than its diff:
```python
import functools
import jax
import jax.numpy as jnp
from jax import lax
from jax.experimental import pallas as pl
from jax.experimental.pallas import tpu as pltpu
from jax.sharding import PartitionSpec as P

HD = 128
BQ = 256
LOG2E = 1.4426950408889634
SCALE = HD ** -0.5
NT = (((1,), (1,)), ((), ()))
NN = (((1,), (0,)), ((), ()))
NEG = -1e30
VMEM = 60 * 2 ** 20
MESH_ID = pl.DeviceIdType.MESH


def mm(a, b, dims):
    return lax.dot_general(a, b, dims, preferred_element_type=jnp.float32)


def gather_kernel(units, w_ref, out_ref, buf, zs, zr, xs, xr, ys, yr, cs, cr, ls, lo):
    x = lax.axis_index('dp')
    z = lax.axis_index('tp')
    cp = lax.axis_index('cp')
    y = cp // 2
    c = cp % 2
    hz = z // 2
    rows = w_ref.shape[0]
    pr = rows // 8
    ur = pr // units
    dx = (1 - x, z, cp)
    dy = (x, z, (1 - y) * 2 + c)
    dc = (x, z, y * 2 + 1 - c)
    src = [1 - z + 4 * hz, 2 - hz, 3 - 3 * hz]
    bar = pltpu.get_barrier_semaphore()
    for d in [(x, src[0], cp), (x, src[1], cp), (x, src[2], cp), dx, dy, dc]:
        pl.semaphore_signal(bar, inc=1, device_id=d, device_id_type=MESH_ID)
    pl.semaphore_wait(bar, 6)

    def eid(xx, yy, cc):
        return (xx * 2 + yy) * 2 + cc

    def un(s, e, u):
        return out_ref.at[s, pl.ds(pl.multiple_of(e * pr + u * ur, 8), ur), :]

    def rc(a, b, ss, rr, dev):
        return pltpu.make_async_remote_copy(src_ref=a, dst_ref=b, send_sem=ss, recv_sem=rr, device_id=dev,
                                            device_id_type=MESH_ID)

    e0, ex, ey, ed = eid(x, y, c), eid(1 - x, y, c), eid(x, 1 - y, c), eid(1 - x, 1 - y, c)
    zsend = []
    for u in range(units):
        for k in range(3):
            q = rc(w_ref.at[pl.ds(pl.multiple_of(e0 * pr + u * ur, 8), ur), :], un(z, e0, u), zs.at[k, u],
                   zr.at[z, u], (x, src[k], cp))
            q.start()
            zsend.append(q)
    nb = 8
    br = rows // nb

    def inb(i):
        return pltpu.make_async_copy(w_ref.at[pl.ds(i * br, br), :], buf.at[i % 2], ls.at[i % 2])

    def outb(i):
        return pltpu.make_async_copy(buf.at[i % 2], out_ref.at[z, pl.ds(i * br, br), :], lo.at[i % 2])

    inb(0).start()
    for i in range(nb):
        inb(i).wait()
        if i >= 1:
            outb(i - 1).wait()
        if i + 1 < nb:
            inb(i + 1).start()
        outb(i).start()
    outb(nb - 1).wait()

    order = [(u, k) for u in range(units) for k in range(3)]
    n = len(order)
    zrecv, xc, yc, fc, cc = [], [], [], [], []
    for i, (u, k) in enumerate(order):
        s = src[k]
        zrecv.append(rc(un(s, e0, u), un(s, e0, u), zs.at[k, u], zr.at[s, u], (x, s, cp)))
        xc.append(rc(un(s, e0, u), un(s, e0, u), xs.at[i, 0], xr.at[i, 0], dx))
        yc.append(rc(un(s, e0, u), un(s, e0, u), ys.at[i, 0], yr.at[i, 0], dy))
        if i % 2 == 0:
            fc.append(rc(un(s, ex, u), un(s, ex, u), ys.at[i, 1], yr.at[i, 1], dy))
        else:
            fc.append(rc(un(s, ey, u), un(s, ey, u), xs.at[i, 1], xr.at[i, 1], dx))
        cc.append([rc(un(s, e, u), un(s, e, u), cs.at[i, j], cr.at[i, j], dc) for j, e in enumerate((e0, ex, ey, ed))])

    def st1(i):
        zrecv[i].wait_recv()
        first, second = (xc, yc) if i % 2 == 0 else (yc, xc)
        first[i].start()
        second[i].start()
        cc[i][0].start()

    def st2(i):
        first = xc if i % 2 == 0 else yc
        first[i].wait_recv()
        fc[i].start()
        cc[i][1 if i % 2 == 0 else 2].start()

    def st3(i):
        second = yc if i % 2 == 0 else xc
        second[i].wait_recv()
        cc[i][2 if i % 2 == 0 else 1].start()

    def st4(i):
        fc[i].wait_recv()
        cc[i][3].start()

    for i in range(n + 3):
        if i < n:
            st1(i)
        if 0 <= i - 1 < n:
            st2(i - 1)
        if 0 <= i - 2 < n:
            st3(i - 2)
        if 0 <= i - 3 < n:
            st4(i - 3)
    for q in zsend:
        q.wait_send()
    for i in range(n):
        for q in [xc[i], yc[i], fc[i]] + cc[i]:
            q.wait_send()
        for q in cc[i]:
            q.wait_recv()


def gather(w, cid, units):
    rows, cols = w.shape
    dma = pltpu.SemaphoreType.DMA
    n = 3 * units
    return pl.pallas_call(
        functools.partial(gather_kernel, units),
        out_shape=jax.ShapeDtypeStruct((4, rows, cols), w.dtype),
        in_specs=[pl.BlockSpec(memory_space=pltpu.HBM)],
        out_specs=pl.BlockSpec(memory_space=pltpu.HBM),
        scratch_shapes=[pltpu.VMEM((2, rows // 8, cols), w.dtype), dma((3, units)), dma((4, units)), dma((n, 2)),
                        dma((n, 2)), dma((n, 2)), dma((n, 2)), dma((n, 4)), dma((n, 4)), dma((2,)), dma((2,))],
        name=f"gather{cid}",
        compiler_params=pltpu.CompilerParams(collective_id=cid, has_side_effects=True, vmem_limit_bytes=VMEM),
        cost_estimate=pl.CostEstimate(flops=10 ** 11, bytes_accessed=10 ** 7, transcendentals=0))(w)


def qkv_kernel(x_ref, w_ref, q_ref, kv_ref):
    r = mm(x_ref[...], w_ref[0], NN).astype(jnp.bfloat16)
    nq = q_ref.shape[2]
    q_ref[0] = r[:, :nq]
    kv_ref[0] = r[:, nq:]


def qkv_proj(x, wqkv):
    rows, d = x.shape
    ng, _, cols = wqkv.shape
    nq = cols - 2 * HD
    return pl.pallas_call(
        qkv_kernel, grid=(ng,),
        out_shape=[jax.ShapeDtypeStruct((ng, rows, nq), jnp.bfloat16), jax.ShapeDtypeStruct((ng, rows, 2 * HD), jnp.bfloat16)],
        in_specs=[pl.BlockSpec((rows, d), lambda g: (0, 0)), pl.BlockSpec((1, d, cols), lambda g: (g, 0, 0))],
        out_specs=[pl.BlockSpec((1, rows, nq), lambda g: (g, 0, 0)), pl.BlockSpec((1, rows, 2 * HD), lambda g: (g, 0, 0))],
        name="qkv_proj", compiler_params=pltpu.CompilerParams(vmem_limit_bytes=VMEM),
        cost_estimate=pl.CostEstimate(flops=2 * rows * d * cols * ng, bytes_accessed=40 * 10 ** 6, transcendentals=0))(x, wqkv)


def do_kernel(x_ref, w_ref, o_ref):
    o_ref[0] = mm(x_ref[...], w_ref[0], NT).astype(jnp.bfloat16)


def do_proj(dy, wo):
    rows, d = dy.shape
    ng, nq, _ = wo.shape
    return pl.pallas_call(
        do_kernel, grid=(ng,),
        out_shape=jax.ShapeDtypeStruct((ng, rows, nq), jnp.bfloat16),
        in_specs=[pl.BlockSpec((rows, d), lambda g: (0, 0)), pl.BlockSpec((1, nq, d), lambda g: (g, 0, 0))],
        out_specs=pl.BlockSpec((1, rows, nq), lambda g: (g, 0, 0)),
        name="do_proj", compiler_params=pltpu.CompilerParams(vmem_limit_bytes=VMEM),
        cost_estimate=pl.CostEstimate(flops=2 * rows * d * nq * ng, bytes_accessed=30 * 10 ** 6, transcendentals=0))(dy, wo)


def y_kernel(o_ref, w_ref, y_ref):
    acc = mm(o_ref[0], w_ref[0], NN)
    for g in range(1, o_ref.shape[0]):
        acc = acc + mm(o_ref[g], w_ref[g], NN)
    y_ref[...] = acc.astype(jnp.bfloat16)


def y_proj(o, wo):
    ng, rows, nq = o.shape
    d = wo.shape[2]
    bn = 512
    return pl.pallas_call(
        y_kernel, grid=(d // bn,),
        out_shape=jax.ShapeDtypeStruct((rows, d), jnp.bfloat16),
        in_specs=[pl.BlockSpec((ng, rows, nq), lambda j: (0, 0, 0)), pl.BlockSpec((ng, nq, bn), lambda j: (0, 0, j))],
        out_specs=pl.BlockSpec((rows, bn), lambda j: (0, j)),
        name="y_proj", compiler_params=pltpu.CompilerParams(vmem_limit_bytes=VMEM),
        cost_estimate=pl.CostEstimate(flops=2 * rows * d * nq * ng, bytes_accessed=30 * 10 ** 6, transcendentals=0))(o, wo)


def dx_kernel(dq_ref, dkv_ref, w_ref, dx_ref):
    nq = dq_ref.shape[2]
    acc = None
    for g in range(dq_ref.shape[0]):
        t = mm(dq_ref[g], w_ref[g, :, :nq], NT) + mm(dkv_ref[g], w_ref[g, :, nq:], NT)
        acc = t if acc is None else acc + t
    dx_ref[...] = acc.astype(jnp.bfloat16)


def dx_proj(dq, dkv, wqkv):
    ng, rows, nq = dq.shape
    _, d, cols = wqkv.shape
    bn = 512
    return pl.pallas_call(
        dx_kernel, grid=(d // bn,),
        out_shape=jax.ShapeDtypeStruct((rows, d), jnp.bfloat16),
        in_specs=[pl.BlockSpec((ng, rows, nq), lambda j: (0, 0, 0)), pl.BlockSpec((ng, rows, 2 * HD), lambda j: (0, 0, 0)),
                  pl.BlockSpec((ng, bn, cols), lambda j: (0, j, 0))],
        out_specs=pl.BlockSpec((rows, bn), lambda j: (0, j)),
        name="dx_proj", compiler_params=pltpu.CompilerParams(vmem_limit_bytes=VMEM),
        cost_estimate=pl.CostEstimate(flops=2 * rows * d * cols * ng, bytes_accessed=40 * 10 ** 6, transcendentals=0))(dq, dkv, wqkv)


def piece_row(j, piece, n_pieces):
    half = n_pieces // 2
    return jnp.where(j < half, j * 2 * piece, (n_pieces - 1 - j) * 2 * piece + piece)


def key_loop(n, piece, n_pieces, tile):
    per = piece // BQ
    full = n // per

    def whole(j, _):
        tile(pl.multiple_of(piece_row(j, piece, n_pieces), BQ), piece, False)
        return 0

    def part(j, _):
        tile(pl.multiple_of(piece_row(full, piece, n_pieces) + (j - full * per) * BQ, BQ), BQ, False)
        return 0

    lax.fori_loop(0, full, whole, 0)
    lax.fori_loop(full * per, n, part, 0)
    tile(pl.multiple_of(piece_row(full, piece, n_pieces) + (n - full * per) * BQ, BQ), BQ, True)


def keep_mask(size):
    r = lax.broadcasted_iota(jnp.int32, (size, BQ), 0)
    q = lax.broadcasted_iota(jnp.int32, (size, BQ), 1)
    return r <= q


def fwd_kernel(nh, piece, n_pieces, pos_ref, q_ref, kv_ref, o_ref, lse_ref, vt_ref, m_ref, l_ref, acc_ref):
    i = pl.program_id(0)
    n = pos_ref[i]

    @pl.when(i == 0)
    def _():
        for b in range(n_pieces):
            vt_ref[:, b * piece:(b + 1) * piece] = kv_ref[b * piece:(b + 1) * piece, HD:].T

    m_ref[...] = jnp.full_like(m_ref, NEG)
    l_ref[...] = jnp.zeros_like(l_ref)
    acc_ref[...] = jnp.zeros_like(acc_ref)

    def tile(start, size, masked):
        k = kv_ref[pl.ds(start, size), :HD]
        vt = vt_ref[:, pl.ds(start, size)]
        scores = [mm(k, q_ref[:, h * HD:(h + 1) * HD], NT) for h in range(nh)]
        for h in range(nh):
            s = scores[h] * (SCALE * LOG2E)
            if masked:
                s = jnp.where(keep_mask(size), s, NEG)
            m_old = m_ref[h:h + 1, :]
            m_new = jnp.maximum(m_old, jnp.max(s, axis=0, keepdims=True))
            p = jnp.exp2(s - m_new)
            a = jnp.exp2(m_old - m_new)
            m_ref[h:h + 1, :] = m_new
            l_ref[h:h + 1, :] = l_ref[h:h + 1, :] * a + jnp.sum(p, axis=0, keepdims=True)
            o = mm(vt, p.astype(jnp.bfloat16), NN)
            acc_ref[h * HD:(h + 1) * HD, :] = acc_ref[h * HD:(h + 1) * HD, :] * a + o

    key_loop(n, piece, n_pieces, tile)
    for h in range(nh):
        l = l_ref[h:h + 1, :]
        o = acc_ref[h * HD:(h + 1) * HD, :] / l
        o_ref[:, h * HD:(h + 1) * HD] = o.T.astype(jnp.bfloat16)
        lse_ref[0, h:h + 1, :] = m_ref[h:h + 1, :] + jnp.log2(l)


def attn_fwd(pos, q, kv, piece):
    rows, width = q.shape
    nh = width // HD
    keys = kv.shape[0]
    nq = rows // BQ
    gs = pltpu.PrefetchScalarGridSpec(
        num_scalar_prefetch=1, grid=(nq,),
        in_specs=[pl.BlockSpec((BQ, width), lambda i, p: (i, 0)), pl.BlockSpec((keys, 2 * HD), lambda i, p: (0, 0))],
        out_specs=[pl.BlockSpec((BQ, width), lambda i, p: (i, 0)), pl.BlockSpec((1, 8, BQ), lambda i, p: (i, 0, 0))],
        scratch_shapes=[pltpu.VMEM((HD, keys), jnp.bfloat16), pltpu.VMEM((8, BQ), jnp.float32),
                        pltpu.VMEM((8, BQ), jnp.float32), pltpu.VMEM((width, BQ), jnp.float32)])
    return pl.pallas_call(
        functools.partial(fwd_kernel, nh, piece, keys // piece),
        out_shape=[jax.ShapeDtypeStruct(q.shape, jnp.bfloat16), jax.ShapeDtypeStruct((nq, 8, BQ), jnp.float32)],
        grid_spec=gs, name="attn_fwd", compiler_params=pltpu.CompilerParams(vmem_limit_bytes=VMEM),
        cost_estimate=pl.CostEstimate(flops=64 * 10 ** 9, bytes_accessed=10 ** 7, transcendentals=0))(pos, q, kv)


def bwd_kernel(nh, piece, n_pieces, pos_ref, q_ref, do_ref, o_ref, lse_ref, kv_ref, dq_ref, dkv_ref, kt_ref, del_ref, dqt_ref):
    i = pl.program_id(0)
    n = pos_ref[i]

    @pl.when(i == 0)
    def _():
        dkv_ref[...] = jnp.zeros_like(dkv_ref)
        for b in range(n_pieces):
            kt_ref[:, b * piece:(b + 1) * piece] = kv_ref[b * piece:(b + 1) * piece, :HD].T

    for h in range(nh):
        sl = slice(h * HD, (h + 1) * HD)
        pr = do_ref[:, sl].astype(jnp.float32) * o_ref[:, sl].astype(jnp.float32)
        del_ref[h:h + 1, :] = jnp.sum(pr.T, axis=0, keepdims=True)
    dqt_ref[...] = jnp.zeros_like(dqt_ref)

    def tile(start, size, masked):
        for t0 in range(0, size, BQ):
            sub(start + t0, masked)

    def sub(start, masked):
        size = BQ
        k = kv_ref[pl.ds(start, size), :HD]
        v = kv_ref[pl.ds(start, size), HD:]
        kt = kt_ref[:, pl.ds(start, size)]
        dv = None
        dk = None
        for h in range(nh):
            sl = slice(h * HD, (h + 1) * HD)
            s = mm(k, q_ref[:, sl], NT) * (SCALE * LOG2E) - lse_ref[0, h:h + 1, :]
            dp = mm(v, do_ref[:, sl], NT)
            if masked:
                s = jnp.where(keep_mask(size), s, NEG)
            pb = jnp.exp2(s).astype(jnp.bfloat16)
            ds = (pb.astype(jnp.float32) * (dp - del_ref[h:h + 1, :])).astype(jnp.bfloat16)
            dvh = mm(pb, do_ref[:, sl], NN)
            dkh = mm(ds, q_ref[:, sl], NN)
            dv = dvh if dv is None else dv + dvh
            dk = dkh if dk is None else dk + dkh
            dqt_ref[sl, :] += mm(kt, ds, NN)
        dkv_ref[pl.ds(start, size), :HD] += dk * SCALE
        dkv_ref[pl.ds(start, size), HD:] += dv

    key_loop(n, piece, n_pieces, tile)
    for h in range(nh):
        sl = slice(h * HD, (h + 1) * HD)
        dq_ref[:, sl] = (dqt_ref[sl, :] * SCALE).T.astype(jnp.bfloat16)


def attn_bwd(pos, q, do, o, lse, kv, piece):
    rows, width = q.shape
    nh = width // HD
    keys = kv.shape[0]
    nq = rows // BQ
    row = pl.BlockSpec((BQ, width), lambda i, p: (i, 0))
    gs = pltpu.PrefetchScalarGridSpec(
        num_scalar_prefetch=1, grid=(nq,),
        in_specs=[row, row, row, pl.BlockSpec((1, 8, BQ), lambda i, p: (i, 0, 0)),
                  pl.BlockSpec((keys, 2 * HD), lambda i, p: (0, 0))],
        out_specs=[row, pl.BlockSpec((keys, 2 * HD), lambda i, p: (0, 0))],
        scratch_shapes=[pltpu.VMEM((HD, keys), jnp.bfloat16), pltpu.VMEM((8, BQ), jnp.float32),
                        pltpu.VMEM((width, BQ), jnp.float32)])
    return pl.pallas_call(
        functools.partial(bwd_kernel, nh, piece, keys // piece),
        out_shape=[jax.ShapeDtypeStruct(q.shape, jnp.bfloat16), jax.ShapeDtypeStruct((keys, 2 * HD), jnp.float32)],
        grid_spec=gs, name="attn_bwd", compiler_params=pltpu.CompilerParams(vmem_limit_bytes=VMEM),
        cost_estimate=pl.CostEstimate(flops=150 * 10 ** 9, bytes_accessed=10 ** 7, transcendentals=0))(pos, q, do, o, lse, kv)


def solution(mesh):
    cp_size = mesh.shape['cp']
    row_spec = P(('dp', 'cp', 'tp'), None)

    def local_step(x_blk, dy_blk, w_query, w_key, w_value, w_out):
        rows, d = x_blk.shape
        ng = mesh.shape['tp']
        seq_loc = rows * ng
        piece = seq_loc // 2
        width = w_query.shape[1]
        rank = lax.axis_index('cp')
        half = piece // BQ
        t = jnp.arange(2 * half, dtype=jnp.int32)
        pos = jnp.where(t < half, rank * half + t, (2 * cp_size - 1 - rank) * half + t - half).astype(jnp.int32)

        def a2a(v):
            return lax.all_to_all(v, 'tp', 0, 0, tiled=True)

        wqkv = gather(jnp.concatenate([w_query, w_key, w_value], axis=1), 1, 4)
        q_g, kv_g = qkv_proj(x_blk, wqkv)
        kv_loc = a2a(kv_g).reshape(seq_loc, 2 * HD)
        kv_all = lax.all_gather(kv_loc, 'cp', axis=0, tiled=True)
        q_loc = a2a(q_g).reshape(seq_loc, width)
        w_out, q_g = lax.optimization_barrier((w_out, q_g))
        wo = gather(w_out, 2, 7)
        do_g = do_proj(dy_blk, wo)
        do_loc = a2a(do_g).reshape(seq_loc, width)
        o_loc, lse = attn_fwd(pos, q_loc, kv_all, piece)
        o_g = a2a(o_loc.reshape(ng, rows, width))
        dq_loc, dkv = attn_bwd(pos, q_loc, do_loc, o_loc, lse, kv_all, piece)
        y_blk = y_proj(o_g, wo)
        dq_g = a2a(dq_loc.reshape(ng, rows, width))
        dkv_own = lax.psum_scatter(dkv, 'cp', scatter_dimension=0, tiled=True).astype(jnp.bfloat16)
        dkv_g = a2a(dkv_own.reshape(ng, rows, 2 * HD))
        dx_blk = dx_proj(dq_g, dkv_g, wqkv)
        return y_blk, dx_blk

    return jax.shard_map(local_step, mesh=mesh, in_specs=(row_spec, row_spec, P(None, 'tp'), P(None, 'tp'), P(None, 'tp'), P('tp', None)),
                         out_specs=(row_spec, row_spec), check_vma=False)
```

time: 1990 us -> 794 us (0.40)
  waiting for transfers between devices: 1110 us -> 83.6 us
  matrix products: 611 us -> 0 us
  Pallas kernels: 0 us -> 596 us
  other arithmetic: 158 us -> 9.99 us
  local copies, waits for them, and re-layouts: 85.5 us -> 2.69 us
  blocking collectives: 0 us -> 65.9 us
    reduce_scatter x4 -> x1, waiting for transfers between devices: 724 us -> 0.02 us  [local_step(): lax.psum_scatter(dkv, 'cp', scatter_dimension=0, tiled=True)]
    dot_general x152 -> x0, matrix products: 611 us -> none  [the longest x24 116 us: block_step(): jnp.einsum('hgqk,khd->qhgd', prob_bf, values_all, preferred_element_type=...]
    pallas_call x0 -> x8, Pallas kernels: none -> 596 us  [the longest x2 321 us: gather(): pl.pallas_call(functools.partial(gather_kernel, units), out_shape=jax.Sha...]
    all_gather x4 -> x1, waiting for transfers between devices: 382 us -> 0.02 us  [local_step(): kv_all = lax.all_gather(kv_loc, 'cp', axis=0, tiled=True)]
    convert_element_type x26 -> x1, other arithmetic: 111 us -> 2.36 us  [local_step(): lax.psum_scatter(dkv, 'cp', scatter_dimension=0, tiled=True)]
    all_to_all x0 -> x5, waiting for transfers between devices: none -> 82.9 us  [a2a(): return lax.all_to_all(v, 'tp', 0, 0, tiled=True)]
    all_to_all x0 -> x1, blocking collectives: none -> 65.9 us  [a2a(): return lax.all_to_all(v, 'tp', 0, 0, tiled=True)]
    while x242 -> x0, local copies, waits for them, and re-layouts: 48.5 us -> none
  transfers between devices with their start and end apart: 8 -> 7, of which waited for: 5 -> 4; matrix products, arithmetic and copies ran while one was open for 8% -> 0% of each run, Pallas kernels for 0% -> 35%
where the time goes in v1:
time: 794 us; the launch traced here: 792 us
  Pallas kernels  596 us (75%)
  waiting for transfers between devices  83.6 us (11%)
  blocking collectives  65.9 us (8%)
  starting transfers between devices  19.3 us (2%)
  between operations  14.1 us (2%)
  other arithmetic  9.99 us (1%)
    pallas_call x2, Pallas kernels, gather(): pl.pallas_call(functools.partial(gather_kernel, units), out_shape=jax.Sha...  321 us
    pallas_call x1, Pallas kernels, attn_bwd(): pl.pallas_call(functools.partial(bwd_kernel, nh, piece, keys // piece), o...  139 us
    all_to_all x5, waiting for transfers between devices, a2a(): return lax.all_to_all(v, 'tp', 0, 0, tiled=True)  82.9 us
    all_to_all x1, blocking collectives, a2a(): return lax.all_to_all(v, 'tp', 0, 0, tiled=True)  65.9 us
    pallas_call x1, Pallas kernels, attn_fwd(): pl.pallas_call(functools.partial(fwd_kernel, nh, piece, keys // piece), o...  61.3 us
    pallas_call x1, Pallas kernels, dx_proj(): pl.pallas_call(dx_kernel, grid=(d // bn,), out_shape=jax.ShapeDtypeStruct...  20.5 us
    pallas_call x1, Pallas kernels, qkv_proj(): pl.pallas_call(qkv_kernel, grid=(ng,), out_shape=[jax.ShapeDtypeStruct((n...  20 us
    all_to_all x5, starting transfers between devices, a2a(): return lax.all_to_all(v, 'tp', 0, 0, tiled=True)  19 us
  transfers between devices with their start and end apart: 7, of which 4 were waited for; matrix products, arithmetic and copies ran while one was open for 0% of the time, Pallas kernels for 35%

profile of v1, /device:TPU:0, one launch (start us, length us, event | category | flops | bytes accessed | tf_op | source)
XLA Modules:
  0.0 792.1 jit_solution(15170166351024427485)
XLA Ops:
  7.2 7.1 pad_maximum_fusion.w_ref
  14.3 138.6 %gather1.1.w_ref = bf16[4,3584,1152]{2,1,0:T(8,128)(2,1)} custom-call(bf16[3584,1152]{1,0:T(8,128)(2,1)} %pad_maximum_fusion.w_ref), custom_call_target="tpu_custom_call" | custom-call | flops 99999997952 | bytes 10000000 | tf_op jit(solution)/shard_map/gather1/pallas_call | solution.py:138
  152.9 20.0 %qkv_proj.1 = (bf16[4,384,896]{2,1,0:T(8,128)(2,1)}, bf16[4,384,256]{2,1,0:T(8,128)(2,1)}) custom-call(bf16[384,3584]{1,0:T(8,128)(2,1)} %x_ref.2, bf16[4,3584,1152]{2,1,0:T(8,128)(2,1)} %gather1.1.w_ref), custom_call_target="tpu_custom_call" | custom-call | flops 12683575296 | bytes 40000000 | tf_op jit(solution)/shard_map/qkv_proj/pallas_call | solution.py:161
  172.9 3.6 all-to-all-start.1
  176.5 20.5 %all-to-all-done.1 = bf16[4,384,256]{2,1,0:T(8,128)(2,1)S(1)} async-done(((bf16[4,384,256]{2,1,0:T(8,128)(2,1)}), bf16[4,384,256]{2,1,0:T(8,128)(2,1)S(1)}, u32[]{:S(2)}, u32[]{:S(2)}) %all-to-all-start.1) | async-done | bytes 786464 | tf_op jit(solution)/shard_map/all_to_all | solution.py:398
  197.0 0.0 copy-start
  197.0 3.7 all-to-all-start
  200.6 0.0 all-gather.2.cloned.1.call-start
  200.7 0.0 copy-done
  200.7 0.7 all-gather.2.cloned.1.call-update
  201.4 182.8 %gather2.1.w_ref = bf16[4,896,3584]{2,1,0:T(8,128)(2,1)} custom-call(bf16[896,3584]{1,0:T(8,128)(2,1)} %w_ref), custom_call_target="tpu_custom_call" | custom-call | flops 99999997952 | bytes 10000000 | tf_op jit(solution)/shard_map/gather2/pallas_call | solution.py:138
  384.2 0.5 compare_select_fusion.pos_ref
  384.8 16.7 %do_proj.1 = bf16[4,384,896]{2,1,0:T(8,128)(2,1)} custom-call(bf16[384,3584]{1,0:T(8,128)(2,1)} %x_ref.3, bf16[4,896,3584]{2,1,0:T(8,128)(2,1)} %gather2.1.w_ref), custom_call_target="tpu_custom_call" | custom-call | flops 9865003008 | bytes 30000000 | tf_op jit(solution)/shard_map/do_proj/pallas_call | solution.py:177
  401.4 0.0 all-to-all-done
  401.4 0.0 copy-start.1
  401.4 4.6 all-to-all-start.3
  406.0 0.2 reduce-scatter.2.cloned.1.call-start
  406.2 0.0 all-gather.2.cloned.1.call-done.kv_ref
  406.3 0.0 copy-done.1
  406.3 61.3 %attn_fwd.1 = (bf16[1536,896]{1,0:T(8,128)(2,1)}, f32[6,8,256]{2,1,0:T(8,128)}) custom-call(s32[6]{0:T(128)} %compare_select_fusion.pos_ref, bf16[1536,896]{1,0:T(8,128)(2,1)} %bitcast.7, bf16[6144,256]{1,0:T(8,128)(2,1)} %all-gather.2.cloned.1.call-done.kv_ref), custom_call_target="tpu_custom_call" | custom-call | flops 64000000000 | bytes 10000000 | tf_op jit(solution)/shard_map/attn_fwd/pallas_call | solution.py:306
  467.5 1.1 all-to-all-done.3
  468.6 139.2 %attn_bwd.1 = (bf16[1536,896]{1,0:T(8,128)(2,1)}, f32[6144,256]{1,0:T(8,128)}) custom-call(s32[6]{0:T(128)} %compare_select_fusion.pos_ref, bf16[1536,896]{1,0:T(8,128)(2,1)} %bitcast.8, bf16[1536,896]{1,0:T(8,128)(2,1)} %bitcast.3.do_ref, bf16[1536,896]{1,0:T(8,128)(2,1)} %get-tuple-element.11.o_ref, f32[6,8,256]{2,1,0:T(8,128)} %get-tuple-element.13.lse_ref, ...), custom_call_target="tpu_custom_call" | custom-call | flops 149999992832 | bytes 10000000 | tf_op jit(solution)/shard_map/attn_bwd/pallas_call | solution.py:375
  607.8 0.0 copy-start.3
  607.8 0.0 reduce-scatter.2.cloned.1.call-update
  607.8 1.8 copy-done.3
  609.6 65.9 %all_to_all.30.o_ref = bf16[4,384,896]{2,1,0:T(8,128)(2,1)} all-to-all(bf16[4,384,896]{2,1,0:T(8,128)(2,1)S(1)} %bitcast.10), channel_id=1, replica_groups=mesh['dp'=2,'tp'=4,'cp'=4] {'tp'}, dimensions={0} | all-to-all | bytes 5505024 | tf_op jit(solution)/shard_map/all_to_all | solution.py:398
  675.5 3.7 all-to-all-start.4
  679.2 0.0 reduce-scatter.2.cloned.1.call-done
  679.2 2.4 convert_element_type.3
  681.6 59.3 %all-to-all-done.4.dq_ref = bf16[4,384,896]{2,1,0:T(8,128)(2,1)S(1)} async-done(((bf16[4,384,896]{2,1,0:T(8,128)(2,1)}), bf16[4,384,896]{2,1,0:T(8,128)(2,1)S(1)}, u32[]{:S(2)}, u32[]{:S(2)}) %all-to-all-start.4) | async-done | bytes 2752544 | tf_op jit(solution)/shard_map/all_to_all | solution.py:398
  740.9 0.0 copy-start.2
  740.9 3.5 all-to-all-start.5
  744.4 17.4 %y_proj.1 = bf16[384,3584]{1,0:T(8,128)(2,1)} custom-call(bf16[4,384,896]{2,1,0:T(8,128)(2,1)} %all_to_all.30.o_ref, bf16[4,896,3584]{2,1,0:T(8,128)(2,1)} %gather2.1.w_ref), custom_call_target="tpu_custom_call" | custom-call | flops 9865003008 | bytes 30000000 | tf_op jit(solution)/shard_map/y_proj/pallas_call | solution.py:197
  761.8 0.0 copy-done.2
  761.8 2.0 all-to-all-done.5.dkv_ref
  763.8 0.0 copy-start.4
  763.8 0.9 copy-done.4
  764.8 20.5 %dx_proj.1 = bf16[384,3584]{1,0:T(8,128)(2,1)} custom-call(bf16[4,384,896]{2,1,0:T(8,128)(2,1)} %copy-done.2, bf16[4,384,256]{2,1,0:T(8,128)(2,1)} %copy-done.4, bf16[4,3584,1152]{2,1,0:T(8,128)(2,1)} %gather1.1.w_ref), custom_call_target="tpu_custom_call" | custom-call | flops 12683575296 | bytes 40000000 | tf_op jit(solution)/shard_map/dx_proj/pallas_call | solution.py:219
Async XLA Ops:
  172.9 24.1 %all-to-all-start.1 = ((bf16[4,384,256]{2,1,0:T(8,128)(2,1)}), bf16[4,384,256]{2,1,0:T(8,128)(2,1)S(1)}, u32[]{:S(2)}, u32[]{:S(2)}) async-start(bf16[4,384,256]{2,1,0:T(8,128)(2,1)} %get-tuple-element.10), calls=%async_computation.1 | async-start | bytes 1572864 | tf_op jit(solution)/shard_map/all_to_all | solution.py:398
  197.0 3.7 copy-start
  197.0 204.5 %all-to-all-start = ((bf16[4,384,896]{2,1,0:T(8,128)(2,1)}), bf16[4,384,896]{2,1,0:T(8,128)(2,1)S(1)}, u32[]{:S(2)}, u32[]{:S(2)}) async-start(bf16[4,384,896]{2,1,0:T(8,128)(2,1)} %get-tuple-element.9), calls=%async_computation | async-start | bytes 5505024 | tf_op jit(solution)/shard_map/all_to_all | solution.py:398
  200.6 205.6 %all-gather.2.cloned.1.call-start = ((), (), s32[]{:S(2)}) async-start(), calls=%async_computation.7 | async-start | bytes 3932160 | tf_op jit(solution)/shard_map/all_gather | solution.py:403
  401.4 4.8 copy-start.1
  401.4 67.2 %all-to-all-start.3 = ((bf16[4,384,896]{2,1,0:T(8,128)(2,1)}), bf16[4,384,896]{2,1,0:T(8,128)(2,1)}, u32[]{:S(2)}, u32[]{:S(2)}) async-start(bf16[4,384,896]{2,1,0:T(8,128)(2,1)} %do_proj.1), calls=%async_computation.3 | async-start | bytes 5505024 | tf_op jit(solution)/shard_map/all_to_all | solution.py:398
  406.0 273.2 %reduce-scatter.2.cloned.1.call-start = ((), (), s32[]{:S(2)}) async-start(), calls=%async_computation.8 | async-start | bytes 7864320 | tf_op jit(solution)/shard_map/reduce_scatter | solution.py:414
  607.8 1.8 copy-start.3
  675.5 65.4 %all-to-all-start.4 = ((bf16[4,384,896]{2,1,0:T(8,128)(2,1)}), bf16[4,384,896]{2,1,0:T(8,128)(2,1)S(1)}, u32[]{:S(2)}, u32[]{:S(2)}) async-start(bf16[4,384,896]{2,1,0:T(8,128)(2,1)} %bitcast.9), calls=%async_computation.4 | async-start | bytes 5505024 | tf_op jit(solution)/shard_map/all_to_all | solution.py:398
  740.9 21.0 %copy-start.2 = (bf16[4,384,896]{2,1,0:T(8,128)(2,1)}, bf16[4,384,896]{2,1,0:T(8,128)(2,1)S(1)}, u32[]{:S(2)}) copy-start(bf16[4,384,896]{2,1,0:T(8,128)(2,1)S(1)} %all-to-all-done.4.dq_ref) | copy-start | bytes 8257540
  740.9 22.9 %all-to-all-start.5 = ((bf16[4,384,256]{2,1,0:T(8,128)(2,1)}), bf16[4,384,256]{2,1,0:T(8,128)(2,1)S(1)}, u32[]{:S(2)}, u32[]{:S(2)}) async-start(bf16[4,384,256]{2,1,0:T(8,128)(2,1)} %bitcast.5), calls=%async_computation.6 | async-start | bytes 1572864 | tf_op jit(solution)/shard_map/all_to_all | solution.py:398
  763.8 0.9 copy-start.4
Sparse Core Ops, SparseCore 0:
  203.6 28.7 all-gather.1
  608.0 55.5 reduce-scatter.1

commit v2 on v1

--- a/solution.py
+++ b/solution.py
@@ -21,78 +21,105 @@
     return lax.dot_general(a, b, dims, preferred_element_type=jnp.float32)
 
 
-def gather_kernel(units, w_ref, out_ref, buf, zs, zr, xs, xr, ys, yr, cs, cr, ls, lo):
+def inphase_kernel(kind, blocks, x_ref, *refs):
+    nb = len(blocks)
+    n = 3 * nb
+    if kind == 'qkv':
+        (wq, wk, wv, wall, a_loc, kv_all, wbuf, obuf, res, zs, zr, xs, xr, ys, yr, cs, cr, ls, os, rs, rr,
+         kys, kyr, kcs, kcr) = refs
+        width = wq.shape[1]
+    else:
+        (wo, wall, a_loc, wbuf, obuf, res, zs, zr, xs, xr, ys, yr, cs, cr, ls, os, rs, rr) = refs
+        width = wo.shape[0]
     x = lax.axis_index('dp')
     z = lax.axis_index('tp')
     cp = lax.axis_index('cp')
     y = cp // 2
     c = cp % 2
     hz = z // 2
-    rows = w_ref.shape[0]
-    pr = rows // 8
-    ur = pr // units
+    inner = jnp.logical_or(z == 1, z == 2)
+    rows = x_ref.shape[0]
     dx = (1 - x, z, cp)
     dy = (x, z, (1 - y) * 2 + c)
     dc = (x, z, y * 2 + 1 - c)
     src = [1 - z + 4 * hz, 2 - hz, 3 - 3 * hz]
+
+    def dz(s):
+        return (x, s, cp)
+
     bar = pltpu.get_barrier_semaphore()
-    for d in [(x, src[0], cp), (x, src[1], cp), (x, src[2], cp), dx, dy, dc]:
+    for d in [dz(src[0]), dz(src[1]), dz(src[2]), dx, dy, dc]:
         pl.semaphore_signal(bar, inc=1, device_id=d, device_id_type=MESH_ID)
     pl.semaphore_wait(bar, 6)
 
     def eid(xx, yy, cc):
         return (xx * 2 + yy) * 2 + cc
 
-    def un(s, e, u):
-        return out_ref.at[s, pl.ds(pl.multiple_of(e * pr + u * ur, 8), ur), :]
-
-    def rc(a, b, ss, rr, dev):
-        return pltpu.make_async_remote_copy(src_ref=a, dst_ref=b, send_sem=ss, recv_sem=rr, device_id=dev,
+    e0, ex, ey, ed = eid(x, y, c), eid(1 - x, y, c), eid(x, 1 - y, c), eid(1 - x, 1 - y, c)
+
+    def eighth(ref, e, off, size):
+        if kind == 'qkv':
+            pr = ref.shape[0] // 8
+            return ref.at[pl.ds(pl.multiple_of(e * pr, 16), pr), pl.ds(off, size)]
+        pr = size // 8
+        return ref.at[pl.ds(pl.multiple_of(off + e * pr, 16), pr), :]
+
+    def block(ref, off, size):
+        if kind == 'qkv':
+            return ref.at[:, pl.ds(off, size)]
+        return ref.at[pl.ds(off, size), :]
+
+    def own_parts(j):
+        off, size = blocks[j]
+        if kind == 'do':
+            return [(wo, off, off, size)]
+        if off < width:
+            return [(wq, off, off, size)]
+        return [(wk, 0, width, HD), (wv, 0, width + HD, HD)]
+
+    def rc(a, b, ss, rsem, dev):
+        return pltpu.make_async_remote_copy(src_ref=a, dst_ref=b, send_sem=ss, recv_sem=rsem, device_id=dev,
                                             device_id_type=MESH_ID)
 
-    e0, ex, ey, ed = eid(x, y, c), eid(1 - x, y, c), eid(x, 1 - y, c), eid(1 - x, 1 - y, c)
-    zsend = []
-    for u in range(units):
-        for k in range(3):
-            q = rc(w_ref.at[pl.ds(pl.multiple_of(e0 * pr + u * ur, 8), ur), :], un(z, e0, u), zs.at[k, u],
-                   zr.at[z, u], (x, src[k], cp))
+    prim, sec = [], []
+    for j in range(nb):
+        for q, (ref, off, dst, size) in enumerate(own_parts(j)):
+            prim.append(rc(eighth(ref, e0, off, size), eighth(wall.at[z], e0, dst, size), zs.at[q, j], zr.at[z, j], dz(src[0])))
+            sec.append(rc(eighth(ref, e0, off, size), eighth(wall.at[z], e0, dst, size), zs.at[2 + q, j], zr.at[z, j], dz(3 - z)))
+    for q in prim:
+        q.start()
+
+    @pl.when(inner)
+    def _():
+        for q in sec:
             q.start()
-            zsend.append(q)
-    nb = 8
-    br = rows // nb
-
-    def inb(i):
-        return pltpu.make_async_copy(w_ref.at[pl.ds(i * br, br), :], buf.at[i % 2], ls.at[i % 2])
-
-    def outb(i):
-        return pltpu.make_async_copy(buf.at[i % 2], out_ref.at[z, pl.ds(i * br, br), :], lo.at[i % 2])
-
-    inb(0).start()
-    for i in range(nb):
-        inb(i).wait()
-        if i >= 1:
-            outb(i - 1).wait()
-        if i + 1 < nb:
-            inb(i + 1).start()
-        outb(i).start()
-    outb(nb - 1).wait()
-
-    order = [(u, k) for u in range(units) for k in range(3)]
-    n = len(order)
-    zrecv, xc, yc, fc, cc = [], [], [], [], []
-    for i, (u, k) in enumerate(order):
+
+    order = [(j, k) for j in range(nb) for k in range(3)]
+    zrecv, zfwd, xc, yc, fc, cc = [], [], [], [], [], []
+    for i, (j, k) in enumerate(order):
         s = src[k]
-        zrecv.append(rc(un(s, e0, u), un(s, e0, u), zs.at[k, u], zr.at[s, u], (x, s, cp)))
-        xc.append(rc(un(s, e0, u), un(s, e0, u), xs.at[i, 0], xr.at[i, 0], dx))
-        yc.append(rc(un(s, e0, u), un(s, e0, u), ys.at[i, 0], yr.at[i, 0], dy))
+        tgt = 3 - z if k == 0 else (z - 1) * 3
+
+        def un(e, s=s, j=j):
+            return eighth(wall.at[s], e, *blocks[j])
+
+        zrecv.append(rc(un(e0), un(e0), zs.at[4 + k, j], zr.at[s, j], dz(s)))
+        zfwd.append(rc(un(e0), un(e0), zs.at[4 + k, j], zr.at[s, j], dz(tgt)))
+        xc.append(rc(un(e0), un(e0), xs.at[i, 0], xr.at[i, 0], dx))
+        yc.append(rc(un(e0), un(e0), ys.at[i, 0], yr.at[i, 0], dy))
         if i % 2 == 0:
-            fc.append(rc(un(s, ex, u), un(s, ex, u), ys.at[i, 1], yr.at[i, 1], dy))
+            fc.append(rc(un(ex), un(ex), ys.at[i, 1], yr.at[i, 1], dy))
         else:
-            fc.append(rc(un(s, ey, u), un(s, ey, u), xs.at[i, 1], xr.at[i, 1], dx))
-        cc.append([rc(un(s, e, u), un(s, e, u), cs.at[i, j], cr.at[i, j], dc) for j, e in enumerate((e0, ex, ey, ed))])
+            fc.append(rc(un(ey), un(ey), xs.at[i, 1], xr.at[i, 1], dx))
+        cc.append([rc(un(e), un(e), cs.at[i, q], cr.at[i, q], dc) for q, e in enumerate((e0, ex, ey, ed))])
 
     def st1(i):
         zrecv[i].wait_recv()
+
+        @pl.when(inner)
+        def _():
+            zfwd[i].start()
+
         first, second = (xc, yc) if i % 2 == 0 else (yc, xc)
         first[i].start()
         second[i].start()
@@ -113,7 +140,106 @@
         fc[i].wait_recv()
         cc[i][3].start()
 
-    for i in range(n + 3):
+    def load(i):
+        j, k = order[i]
+        return pltpu.make_async_copy(block(wall.at[src[k]], *blocks[j]), block(wbuf.at[i % 2], 0, blocks[j][1]), ls.at[i % 2])
+
+    def st5(i):
+        for q in cc[i]:
+            q.wait_recv()
+        load(i).start()
+
+    def project(buf, slot, j):
+        off, size = blocks[j]
+        if kind == 'qkv':
+            r = mm(x_ref[...], buf[:, :size], NN)
+        else:
+            r = mm(x_ref[...], buf[:size, :], NT)
+        res[slot, :, off:off + size] = r.astype(jnp.bfloat16)
+
+    def arow(t):
+        return pl.ds(pl.multiple_of(t * rows, 8), rows)
+
+    def kvrow(p, t):
+        return kv_all.at[pl.ds(pl.multiple_of((p * 4 + t) * rows, 8), rows), :]
+
+    def result(slot, j, t):
+        off, size = blocks[j]
+        here = res.at[slot, :, pl.ds(off, size)]
+        if off >= width:
+            return here, kvrow(cp, t)
+        return here, a_loc.at[arow(t), pl.ds(off, size)]
+
+    rsend = {(j, k): rc(*result(k, j, z), rs.at[j, k], rr.at[z, j], dz(src[k])) for j, k in order}
+    rrecv = {(j, k): rc(*result(k, j, src[k]), rs.at[j, k], rr.at[src[k], j], dz(src[k])) for j, k in order}
+
+    def st6(i):
+        j, k = order[i]
+        load(i).wait()
+        project(wbuf.at[i % 2], k, j)
+        rsend[j, k].start()
+
+    def own_in(j):
+        return [pltpu.make_async_copy(block(ref, off, size), block(obuf.at[j % 2], dst - blocks[j][0], size), os.at[j % 2, q])
+                for q, (ref, off, dst, size) in enumerate(own_parts(j))]
+
+    def own_out(j):
+        return pltpu.make_async_copy(block(obuf.at[j % 2], 0, blocks[j][1]), block(wall.at[z], *blocks[j]), os.at[j % 2, 2])
+
+    def own_res(j):
+        return pltpu.make_async_copy(*result(3, j, z), os.at[2 + j, 0])
+
+    def own_start(j):
+        if j >= 2:
+            own_out(j - 2).wait()
+        for q in own_in(j):
+            q.start()
+
+    def own_do(j):
+        for q in own_in(j):
+            q.wait()
+        own_out(j).start()
+        project(obuf.at[j % 2], 3, j)
+        own_res(j).start()
+
+    if kind == 'qkv':
+        py = (1 - y) * 2 + c
+        ts = [z] + src
+        kyc = [rc(kvrow(cp, t), kvrow(cp, t), kys.at[j], kyr.at[j], dy) for j, t in enumerate(ts)]
+        kyr_ = [rc(kvrow(py, t), kvrow(py, t), kys.at[j], kyr.at[j], dy) for j, t in enumerate(ts)]
+        kcc = [rc(kvrow(cp, t), kvrow(cp, t), kcs.at[j, 0], kcr.at[j, 0], dc) for j, t in enumerate(ts)]
+        kcf = [rc(kvrow(py, t), kvrow(py, t), kcs.at[j, 1], kcr.at[j, 1], dc) for j, t in enumerate(ts)]
+
+        def kv1(j):
+            if j == 0:
+                own_res(0).wait()
+            else:
+                rrecv[0, j - 1].wait_recv()
+            kyc[j].start()
+            kcc[j].start()
+
+        def kv2(j):
+            kyr_[j].wait_recv()
+            kcf[j].start()
+
+    own_start(0)
+    own_start(1)
+    later = {}
+
+    def at(i, f, *args):
+        later.setdefault(i, []).append(functools.partial(f, *args))
+
+    for j in range(nb):
+        at(3 * j + 1, own_do, j)
+        if j + 2 < nb:
+            at(3 * j + 2, own_start, j + 2)
+    if kind == 'qkv':
+        at(3, kv1, 0)
+        for j in range(1, 4):
+            at(7 + j, kv1, j)
+        for j in range(4):
+            at(9 + j, kv2, j)
+    for i in range(max(n + 6, max(later) + 1)):
         if i < n:
             st1(i)
         if 0 <= i - 1 < n:
@@ -122,65 +248,74 @@
             st3(i - 2)
         if 0 <= i - 3 < n:
             st4(i - 3)
-    for q in zsend:
+        if 0 <= i - 5 < n:
+            st6(i - 5)
+        if 0 <= i - 4 < n:
+            st5(i - 4)
+        for f in later.get(i, []):
+            f()
+
+    for q in prim:
         q.wait_send()
+
+    @pl.when(inner)
+    def _():
+        for q in sec + zfwd:
+            q.wait_send()
+
     for i in range(n):
         for q in [xc[i], yc[i], fc[i]] + cc[i]:
             q.wait_send()
-        for q in cc[i]:
-            q.wait_recv()
-
-
-def gather(w, cid, units):
-    rows, cols = w.shape
+    for j in range(nb):
+        if j >= nb - 2:
+            own_out(j).wait()
+        if not (kind == 'qkv' and j == 0):
+            own_res(j).wait()
+        for k in range(3):
+            rsend[j, k].wait_send()
+            if not (kind == 'qkv' and j == 0):
+                rrecv[j, k].wait_recv()
+    if kind == 'qkv':
+        for j in range(4):
+            kyc[j].wait_send()
+            kcc[j].wait_send()
+            kcf[j].wait_send()
+            kcc[j].wait_recv()
+            kcf[j].wait_recv()
+
+
+def inphase(kind, x, ws, blocks, cid):
+    rows, d = x.shape
+    qkv = kind == 'qkv'
+    cols = sum(w.shape[1] for w in ws) if qkv else ws[0].shape[0]
+    width = cols - 2 * HD if qkv else cols
+    big = max(b[1] for b in blocks)
     dma = pltpu.SemaphoreType.DMA
-    n = 3 * units
+    nb = len(blocks)
+    n = 3 * nb
+    hbm = pl.BlockSpec(memory_space=pltpu.HBM)
+    bf = jnp.bfloat16
+    out_shape = [jax.ShapeDtypeStruct((4, d, cols) if qkv else (4, cols, d), bf), jax.ShapeDtypeStruct((4 * rows, width), bf)]
+    tile = (2, d, big) if qkv else (2, big, d)
+    scratch = [pltpu.VMEM(tile, bf), pltpu.VMEM(tile, bf), pltpu.VMEM((4, rows, cols), bf),
+               dma((7, nb)), dma((4, nb)), dma((n, 2)), dma((n, 2)), dma((n, 2)), dma((n, 2)), dma((n, 4)), dma((n, 4)),
+               dma((2,)), dma((2 + nb, 3)), dma((nb, 3)), dma((4, nb))]
+    if qkv:
+        out_shape.append(jax.ShapeDtypeStruct((16 * rows, 2 * HD), bf))
+        scratch += [dma((4,)), dma((4,)), dma((4, 2)), dma((4, 2))]
     return pl.pallas_call(
-        functools.partial(gather_kernel, units),
-        out_shape=jax.ShapeDtypeStruct((4, rows, cols), w.dtype),
-        in_specs=[pl.BlockSpec(memory_space=pltpu.HBM)],
-        out_specs=pl.BlockSpec(memory_space=pltpu.HBM),
-        scratch_shapes=[pltpu.VMEM((2, rows // 8, cols), w.dtype), dma((3, units)), dma((4, units)), dma((n, 2)),
-                        dma((n, 2)), dma((n, 2)), dma((n, 2)), dma((n, 4)), dma((n, 4)), dma((2,)), dma((2,))],
-        name=f"gather{cid}",
+        functools.partial(inphase_kernel, kind, blocks),
+        out_shape=out_shape,
+        in_specs=[pl.BlockSpec(memory_space=pltpu.VMEM)] + [hbm] * len(ws),
+        out_specs=[hbm] * len(out_shape),
+        scratch_shapes=scratch,
+        name=f"inphase_{kind}",
         compiler_params=pltpu.CompilerParams(collective_id=cid, has_side_effects=True, vmem_limit_bytes=VMEM),
-        cost_estimate=pl.CostEstimate(flops=10 ** 11, bytes_accessed=10 ** 7, transcendentals=0))(w)
-
-
-def qkv_kernel(x_ref, w_ref, q_ref, kv_ref):
-    r = mm(x_ref[...], w_ref[0], NN).astype(jnp.bfloat16)
-    nq = q_ref.shape[2]
-    q_ref[0] = r[:, :nq]
-    kv_ref[0] = r[:, nq:]
-
-
-def qkv_proj(x, wqkv):
-    rows, d = x.shape
-    ng, _, cols = wqkv.shape
-    nq = cols - 2 * HD
-    return pl.pallas_call(
-        qkv_kernel, grid=(ng,),
-        out_shape=[jax.ShapeDtypeStruct((ng, rows, nq), jnp.bfloat16), jax.ShapeDtypeStruct((ng, rows, 2 * HD), jnp.bfloat16)],
-        in_specs=[pl.BlockSpec((rows, d), lambda g: (0, 0)), pl.BlockSpec((1, d, cols), lambda g: (g, 0, 0))],
-        out_specs=[pl.BlockSpec((1, rows, nq), lambda g: (g, 0, 0)), pl.BlockSpec((1, rows, 2 * HD), lambda g: (g, 0, 0))],
-        name="qkv_proj", compiler_params=pltpu.CompilerParams(vmem_limit_bytes=VMEM),
-        cost_estimate=pl.CostEstimate(flops=2 * rows * d * cols * ng, bytes_accessed=40 * 10 ** 6, transcendentals=0))(x, wqkv)
-
-
-def do_kernel(x_ref, w_ref, o_ref):
-    o_ref[0] = mm(x_ref[...], w_ref[0], NT).astype(jnp.bfloat16)
-
-
-def do_proj(dy, wo):
-    rows, d = dy.shape
-    ng, nq, _ = wo.shape
-    return pl.pallas_call(
-        do_kernel, grid=(ng,),
-        out_shape=jax.ShapeDtypeStruct((ng, rows, nq), jnp.bfloat16),
-        in_specs=[pl.BlockSpec((rows, d), lambda g: (0, 0)), pl.BlockSpec((1, nq, d), lambda g: (g, 0, 0))],
-        out_specs=pl.BlockSpec((1, rows, nq), lambda g: (g, 0, 0)),
-        name="do_proj", compiler_params=pltpu.CompilerParams(vmem_limit_bytes=VMEM),
-        cost_estimate=pl.CostEstimate(flops=2 * rows * d * nq * ng, bytes_accessed=30 * 10 ** 6, transcendentals=0))(dy, wo)
+        cost_estimate=pl.CostEstimate(flops=10 ** 11, bytes_accessed=10 ** 7, transcendentals=0))(x, *ws)
+
+
+def split_blocks(total, size):
+    return [(o, min(size, total - o)) for o in range(0, total, size)]
 
 
 def y_kernel(o_ref, w_ref, y_ref):
@@ -397,15 +532,10 @@
         def a2a(v):
             return lax.all_to_all(v, 'tp', 0, 0, tiled=True)
 
-        wqkv = gather(jnp.concatenate([w_query, w_key, w_value], axis=1), 1, 4)
-        q_g, kv_g = qkv_proj(x_blk, wqkv)
-        kv_loc = a2a(kv_g).reshape(seq_loc, 2 * HD)
-        kv_all = lax.all_gather(kv_loc, 'cp', axis=0, tiled=True)
-        q_loc = a2a(q_g).reshape(seq_loc, width)
-        w_out, q_g = lax.optimization_barrier((w_out, q_g))
-        wo = gather(w_out, 2, 7)
-        do_g = do_proj(dy_blk, wo)
-        do_loc = a2a(do_g).reshape(seq_loc, width)
+        qkv_blocks = [(width, 2 * HD)] + split_blocks(width, 256)
+        wqkv, q_loc, kv_all = inphase('qkv', x_blk, [w_query, w_key, w_value], qkv_blocks, 1)
+        w_out, q_loc = lax.optimization_barrier((w_out, q_loc))
+        wo, do_loc = inphase('do', dy_blk, [w_out], split_blocks(width, 256), 2)
         o_loc, lse = attn_fwd(pos, q_loc, kv_all, piece)
         o_g = a2a(o_loc.reshape(ng, rows, width))
         dq_loc, dkv = attn_bwd(pos, q_loc, do_loc, o_loc, lse, kv_all, piece)

time: 794 us -> 701 us (0.88)
  Pallas kernels: 596 us -> 534 us
  waiting for transfers between devices: 83.6 us -> 61.5 us
  starting transfers between devices: 19.3 us -> 7.2 us
    pallas_call x4 -> x2, Pallas kernels: 358 us -> 295 us  [inphase(): pl.pallas_call(functools.partial(inphase_kernel, kind, blocks), out_shape...]
    all_to_all x5 -> x2, waiting for transfers between devices: 82.9 us -> 61.4 us  [a2a(): return lax.all_to_all(v, 'tp', 0, 0, tiled=True)]
    all_to_all x5 -> x2, starting transfers between devices: 19 us -> 7.16 us  [a2a(): return lax.all_to_all(v, 'tp', 0, 0, tiled=True)]
  transfers between devices with their start and end apart: 7 -> 3, of which waited for: 4 -> 2; matrix products, arithmetic and copies ran while one was open for 0% -> 0% of each run, Pallas kernels for 35% -> 3%
where the time goes in v2:
time: 701 us; the launch traced here: 692 us
  Pallas kernels  534 us (76%)
  blocking collectives  69.7 us (10%)
  waiting for transfers between devices  61.5 us (9%)
  between operations  14.5 us (2%)
  starting transfers between devices  7.2 us (1%)
    pallas_call x2, Pallas kernels, inphase(): pl.pallas_call(functools.partial(inphase_kernel, kind, blocks), out_shape...  295 us
    pallas_call x1, Pallas kernels, attn_bwd(): pl.pallas_call(functools.partial(bwd_kernel, nh, piece, keys // piece), o...  139 us
    all_to_all x1, blocking collectives, a2a(): return lax.all_to_all(v, 'tp', 0, 0, tiled=True)  69.7 us
    all_to_all x2, waiting for transfers between devices, a2a(): return lax.all_to_all(v, 'tp', 0, 0, tiled=True)  61.4 us
    pallas_call x1, Pallas kernels, attn_fwd(): pl.pallas_call(functools.partial(fwd_kernel, nh, piece, keys // piece), o...  61.3 us
    pallas_call x1, Pallas kernels, dx_proj(): pl.pallas_call(dx_kernel, grid=(d // bn,), out_shape=jax.ShapeDtypeStruct...  20.5 us
    pallas_call x1, Pallas kernels, y_proj(): pl.pallas_call(y_kernel, grid=(d // bn,), out_shape=jax.ShapeDtypeStruct(...  17.4 us
  transfers between devices with their start and end apart: 3, of which 2 were waited for; matrix products, arithmetic and copies ran while one was open for 0% of the time, Pallas kernels for 3%

profile of v2, /device:TPU:0, one launch (start us, length us, event | category | flops | bytes accessed | tf_op | source)
XLA Modules:
  0.0 692.1 jit_solution(3926285787163724233)
XLA Ops:
  7.2 0.0 reduce-scatter.2.cloned.1.call-start
  7.2 172.2 %inphase_qkv.1 = (bf16[4,3584,1152]{2,1,0:T(8,128)(2,1)}, bf16[1536,896]{1,0:T(8,128)(2,1)}, bf16[6144,256]{1,0:T(8,128)(2,1)}) custom-call(bf16[384,3584]{1,0:T(8,128)(2,1)} %x_ref.2, bf16[3584,896]{1,0:T(8,128)(2,1)} %refs_0_.1, bf16[3584,128]{1,0:T(8,128)(2,1)} %refs_1_.1, bf16[3584,128]{1,0:T(8,128)(2,1)} %refs_2_.1), custom_call_target="tpu_custom_call" | custom-call | flops 99999997952 | bytes 10000000 | tf_op jit(solution)/shard_map/inphase_qkv/pallas_call | solution.py:306
  179.5 0.5 compare_select_fusion.pos_ref
  180.0 123.1 %inphase_do.1 = (bf16[4,896,3584]{2,1,0:T(8,128)(2,1)}, bf16[1536,896]{1,0:T(8,128)(2,1)}) custom-call(bf16[384,3584]{1,0:T(8,128)(2,1)} %x_ref.3, bf16[896,3584]{1,0:T(8,128)(2,1)} %refs_0_.2), custom_call_target="tpu_custom_call" | custom-call | flops 99999997952 | bytes 10000000 | tf_op jit(solution)/shard_map/inphase_do/pallas_call | solution.py:306
  303.1 61.3 %attn_fwd.1 = (bf16[1536,896]{1,0:T(8,128)(2,1)}, f32[6,8,256]{2,1,0:T(8,128)}) custom-call(s32[6]{0:T(128)} %compare_select_fusion.pos_ref, bf16[1536,896]{1,0:T(8,128)(2,1)} %get-tuple-element.14.q_ref, bf16[6144,256]{1,0:T(8,128)(2,1)} %get-tuple-element.15.kv_ref), custom_call_target="tpu_custom_call" | custom-call | flops 64000000000 | bytes 10000000 | tf_op jit(solution)/shard_map/attn_fwd/pallas_call | solution.py:441
  364.4 139.1 %attn_bwd.1 = (bf16[1536,896]{1,0:T(8,128)(2,1)}, f32[6144,256]{1,0:T(8,128)}) custom-call(s32[6]{0:T(128)} %compare_select_fusion.pos_ref, bf16[1536,896]{1,0:T(8,128)(2,1)} %get-tuple-element.14.q_ref, bf16[1536,896]{1,0:T(8,128)(2,1)} %get-tuple-element.19.do_ref, bf16[1536,896]{1,0:T(8,128)(2,1)} %get-tuple-element.16.o_ref, ...), custom_call_target="tpu_custom_call" | custom-call | flops 149999992832 | bytes 10000000 | tf_op jit(solution)/shard_map/attn_bwd/pallas_call | solution.py:510
  503.5 0.0 copy-start.1
  503.5 0.0 reduce-scatter.2.cloned.1.call-update
  503.6 1.8 copy-done.1
  505.3 69.7 %all_to_all.15.o_ref = bf16[4,384,896]{2,1,0:T(8,128)(2,1)} all-to-all(bf16[4,384,896]{2,1,0:T(8,128)(2,1)S(1)} %bitcast.4), channel_id=1, replica_groups=mesh['dp'=2,'tp'=4,'cp'=4] {'tp'}, dimensions={0} | all-to-all | bytes 5505024 | tf_op jit(solution)/shard_map/all_to_all | solution.py:533
  575.0 3.7 all-to-all-start.1
  578.7 0.0 reduce-scatter.2.cloned.1.call-done
  578.7 2.4 convert_element_type.3
  581.1 59.5 %all-to-all-done.1.dq_ref = bf16[4,384,896]{2,1,0:T(8,128)(2,1)S(1)} async-done(((bf16[4,384,896]{2,1,0:T(8,128)(2,1)}), bf16[4,384,896]{2,1,0:T(8,128)(2,1)S(1)}, u32[]{:S(2)}, u32[]{:S(2)}) %all-to-all-start.1) | async-done | bytes 2752544 | tf_op jit(solution)/shard_map/all_to_all | solution.py:533
  640.5 0.0 copy-start
  640.5 3.5 all-to-all-start.2
  644.0 17.4 %y_proj.1 = bf16[384,3584]{1,0:T(8,128)(2,1)} custom-call(bf16[4,384,896]{2,1,0:T(8,128)(2,1)} %all_to_all.15.o_ref, bf16[4,896,3584]{2,1,0:T(8,128)(2,1)} %get-tuple-element.18.w_ref), custom_call_target="tpu_custom_call" | custom-call | flops 9865003008 | bytes 30000000 | tf_op jit(solution)/shard_map/y_proj/pallas_call | solution.py:332
  661.5 0.0 copy-done
  661.5 2.0 all-to-all-done.2.dkv_ref
  663.5 0.0 copy-start.2
  663.5 0.9 copy-done.2
  664.4 20.5 %dx_proj.1 = bf16[384,3584]{1,0:T(8,128)(2,1)} custom-call(bf16[4,384,896]{2,1,0:T(8,128)(2,1)} %copy-done, bf16[4,384,256]{2,1,0:T(8,128)(2,1)} %copy-done.2, bf16[4,3584,1152]{2,1,0:T(8,128)(2,1)} %get-tuple-element.23.w_ref), custom_call_target="tpu_custom_call" | custom-call | flops 12683575296 | bytes 40000000 | tf_op jit(solution)/shard_map/dx_proj/pallas_call | solution.py:354
Async XLA Ops:
  7.2 571.5 %reduce-scatter.2.cloned.1.call-start = ((), (), s32[]{:S(2)}) async-start(), calls=%async_computation.4 | async-start | bytes 7864320 | tf_op jit(solution)/shard_map/reduce_scatter | solution.py:544
  503.5 1.8 copy-start.1
  575.0 65.5 %all-to-all-start.1 = ((bf16[4,384,896]{2,1,0:T(8,128)(2,1)}), bf16[4,384,896]{2,1,0:T(8,128)(2,1)S(1)}, u32[]{:S(2)}, u32[]{:S(2)}) async-start(bf16[4,384,896]{2,1,0:T(8,128)(2,1)} %bitcast.3), calls=%async_computation.1 | async-start | bytes 5505024 | tf_op jit(solution)/shard_map/all_to_all | solution.py:533
  640.5 21.0 %copy-start = (bf16[4,384,896]{2,1,0:T(8,128)(2,1)}, bf16[4,384,896]{2,1,0:T(8,128)(2,1)S(1)}, u32[]{:S(2)}) copy-start(bf16[4,384,896]{2,1,0:T(8,128)(2,1)S(1)} %all-to-all-done.1.dq_ref) | copy-start | bytes 8257540
  640.5 22.9 %all-to-all-start.2 = ((bf16[4,384,256]{2,1,0:T(8,128)(2,1)}), bf16[4,384,256]{2,1,0:T(8,128)(2,1)S(1)}, u32[]{:S(2)}, u32[]{:S(2)}) async-start(bf16[4,384,256]{2,1,0:T(8,128)(2,1)} %bitcast.2), calls=%async_computation.3 | async-start | bytes 1572864 | tf_op jit(solution)/shard_map/all_to_all | solution.py:533
  663.5 0.9 copy-start.2
Sparse Core Ops, SparseCore 0:
  503.7 55.9 reduce-scatter.1

commit v3 on v1

v3 whole, which is shorter than its diff:
```python
import functools
import jax
import jax.numpy as jnp
from jax import lax
from jax.experimental import pallas as pl
from jax.experimental.pallas import tpu as pltpu
from jax.sharding import PartitionSpec as P

HD = 128
BQ = 256
LOG2E = 1.4426950408889634
SCALE = HD ** -0.5
NT = (((1,), (1,)), ((), ()))
NN = (((1,), (0,)), ((), ()))
NEG = -1e30
VMEM = 60 * 2 ** 20
MESH_ID = pl.DeviceIdType.MESH


def mm(a, b, dims):
    return lax.dot_general(a, b, dims, preferred_element_type=jnp.float32)


def input_kernel(piece, n_pieces, x_ref, dy_ref, wq, wk, wv, wo, wqkv_all, wo_all, q_loc, kv_all, do_loc, o_loc, lse_ref,
                 wbuf, vbuf, obuf, pbuf, res, resd, qv, kvv, vt_ref, m_ref, l_ref, acc_ref, ost,
                 zs, zr, xs, xr, ys, yr, cs, cr, ls, os, orr, rs, rr, kys, kyr, kcs, kcr, fs):
    width = wq.shape[1]
    nh = width // HD
    nkv = nh + 2
    nb = nkv + nh
    n = 3 * nb
    x = lax.axis_index('dp')
    z = lax.axis_index('tp')
    cp = lax.axis_index('cp')
    y = cp // 2
    c = cp % 2
    hz = z // 2
    inner = jnp.logical_or(z == 1, z == 2)
    rows = x_ref.shape[0]
    dx = (1 - x, z, cp)
    dy = (x, z, (1 - y) * 2 + c)
    dc = (x, z, y * 2 + 1 - c)
    src = [1 - z + 4 * hz, 2 - hz, 3 - 3 * hz]

    def dz(s):
        return (x, s, cp)

    bar = pltpu.get_barrier_semaphore()
    for d in [dz(src[0]), dz(src[1]), dz(src[2]), dx, dy, dc]:
        pl.semaphore_signal(bar, inc=1, device_id=d, device_id_type=MESH_ID)
    pl.semaphore_wait(bar, 6)

    def eid(xx, yy, cc):
        return (xx * 2 + yy) * 2 + cc

    e0, ex, ey, ed = eid(x, y, c), eid(1 - x, y, c), eid(x, 1 - y, c), eid(1 - x, 1 - y, c)
    dk = wq.shape[0] // 8
    dr = HD // 8

    def by_kind(j, f):
        def qkv():
            f(True, pl.multiple_of(jnp.where(j < 2, width + j * HD, (j - 2) * HD), HD))

        def out():
            f(False, pl.multiple_of((j - nkv) * HD, HD))

        if isinstance(j, int):
            qkv() if j < nkv else out()
        else:
            pl.when(j < nkv)(qkv)
            pl.when(j >= nkv)(out)

    def block(qkv, s, off):
        return wqkv_all.at[s, :, pl.ds(off, HD)] if qkv else wo_all.at[s, pl.ds(off, HD), :]

    def eighth(qkv, s, e, off):
        if qkv:
            return wqkv_all.at[s, pl.ds(pl.multiple_of(e * dk, 16), dk), pl.ds(off, HD)]
        return wo_all.at[s, pl.ds(pl.multiple_of(off + e * dr, 16), dr), :]

    def own_block(j):
        if j < 2:
            return (wk, wv)[j], 0
        return (wq, (j - 2) * HD) if j < nkv else (wo, (j - nkv) * HD)

    def rc(a, b, ss, rsem, dev):
        return pltpu.make_async_remote_copy(src_ref=a, dst_ref=b, send_sem=ss, recv_sem=rsem, device_id=dev,
                                            device_id_type=MESH_ID)

    def own_piece(j):
        ref, off = own_block(j)
        if j < nkv:
            return ref.at[pl.ds(pl.multiple_of(e0 * dk, 16), dk), pl.ds(off, HD)]
        return ref.at[pl.ds(pl.multiple_of(off + e0 * dr, 16), dr), :]

    prim, sec = [], []
    for j in range(nb):
        dst = []
        by_kind(j, lambda qkv, off: dst.append(eighth(qkv, z, e0, off)))
        prim.append(rc(own_piece(j), dst[0], zs.at[0, j], zr.at[z, j], dz(src[0])))
        sec.append(rc(own_piece(j), dst[0], zs.at[1, j], zr.at[z, j], dz(3 - z)))

    def own_send(j0, j1):
        for q in prim[j0:j1]:
            q.start()

        @pl.when(inner)
        def _():
            for q in sec[j0:j1]:
                q.start()

    own_send(0, nkv)

    def unit(i):
        j, k = i // 3, i % 3
        return j, k, jnp.where(k == 0, src[0], jnp.where(k == 1, src[1], src[2]))

    def copies(i, qkv, off):
        j, k, s = unit(i)
        tgt = jnp.where(k == 0, 3 - z, (z - 1) * 3)
        un = functools.partial(eighth, qkv, s, off=off)
        d = dict(zr=rc(un(e0), un(e0), zs.at[2 + k, j], zr.at[s, j], dz(s)),
                 zf=rc(un(e0), un(e0), zs.at[2 + k, j], zr.at[s, j], dz(tgt)),
                 x=rc(un(e0), un(e0), xs.at[i, 0], xr.at[i, 0], dx),
                 y=rc(un(e0), un(e0), ys.at[i, 0], yr.at[i, 0], dy),
                 fy=rc(un(ex), un(ex), ys.at[i, 1], yr.at[i, 1], dy),
                 fx=rc(un(ey), un(ey), xs.at[i, 1], xr.at[i, 1], dx))
        for q, e in enumerate((e0, ex, ey, ed)):
            d[q] = rc(un(e), un(e), cs.at[i, q], cr.at[i, q], dc)
        return d

    def stage(i, f):
        def run(qkv, off):
            d = copies(i, qkv, off)
            pl.when(i % 2 == 0)(functools.partial(f, d, True))
            pl.when(i % 2 == 1)(functools.partial(f, d, False))

        @pl.when(jnp.logical_and(i >= 0, i < n))
        def _():
            by_kind(i // 3, run)

    def st1(d, even):
        d['zr'].wait_recv()

        @pl.when(inner)
        def _():
            d['zf'].start()

        d['x' if even else 'y'].start()
        d['y' if even else 'x'].start()
        d[0].start()

    def st2(d, even):
        d['x' if even else 'y'].wait_recv()
        d['fy' if even else 'fx'].start()
        d[1 if even else 2].start()

    def st3(d, even):
        d['y' if even else 'x'].wait_recv()
        d[2 if even else 1].start()

    def st4(d, even):
        d['fy' if even else 'fx'].wait_recv()
        d[3].start()

    def arow(t):
        return pl.ds(pl.multiple_of(t * rows, 16), rows)

    def kvrow(p, t):
        return pl.ds(pl.multiple_of((p * 4 + t) * rows, 16), rows)

    def project(qkv, buf, slot, off):
        step = rows // 3

        def part(r, _):
            w = pl.ds(pl.multiple_of(r * step, 16), step)
            if qkv:
                res[slot, w, pl.ds(off, HD)] = mm(x_ref[w, :], buf, NN).astype(jnp.bfloat16)
            else:
                resd[slot, w, pl.ds(off, HD)] = mm(dy_ref[w, :], buf, NT).astype(jnp.bfloat16)
            return 0

        lax.fori_loop(0, 3, part, 0)

    def result(j, slot, t, f):
        def run(qkv, off):
            here = (res if qkv else resd).at[slot, :, pl.ds(off, HD)]
            if not qkv:
                f(here, do_loc.at[arow(t), pl.ds(off, HD)])
                return

            @pl.when(j < 2)
            def _():
                f(here, kv_all.at[kvrow(cp, t), pl.ds(pl.multiple_of(j * HD, HD), HD)])

            @pl.when(j >= 2)
            def _():
                f(here, q_loc.at[arow(t), pl.ds(off, HD)])

        by_kind(j, run)

    def load(i, qkv, off):
        _, _, s = unit(i)
        return pltpu.make_async_copy(block(qkv, s, off), (wbuf if qkv else vbuf).at[i % 2], ls.at[i % 2])

    def st5(i):
        @pl.when(jnp.logical_and(i >= 0, i < n))
        def _():
            def run(qkv, off):
                d = copies(i, qkv, off)
                for q in range(4):
                    d[q].wait_recv()
                load(i, qkv, off).start()

            by_kind(i // 3, run)

    def st6(i):
        @pl.when(jnp.logical_and(i >= 0, i < n))
        def _():
            j, k, s = unit(i)

            def run(qkv, off):
                load(i, qkv, off).wait()
                project(qkv, (wbuf if qkv else vbuf)[i % 2], k, off)

            by_kind(j, run)
            result(j, k, z, lambda a, b: rc(a, b, rs.at[j, k], rr.at[z, j], dz(s)).start())

    def own_in(j, f):
        def run(qkv, off):
            buf = (obuf if qkv else pbuf).at[j % 2]
            if not qkv:
                f(pltpu.make_async_copy(wo.at[pl.ds(off, HD), :], buf, os.at[j % 2]))
            elif isinstance(j, int) and j < 2:
                f(pltpu.make_async_copy((wk, wv)[j], buf, os.at[j % 2]))
            else:
                f(pltpu.make_async_copy(wq.at[:, pl.ds(off, HD)], buf, os.at[j % 2]))

        by_kind(j, run)

    def own_do(j):
        own_in(j, lambda q: q.wait())

        def run(qkv, off):
            buf = (obuf if qkv else pbuf)
            keep = pltpu.make_async_copy(buf.at[j % 2], block(qkv, z, off), os.at[2])
            keep.start()
            project(qkv, buf[j % 2], 3, off)
            keep.wait()

        by_kind(j, run)
        result(j, 3, z, lambda a, b: pltpu.make_async_copy(a, b, orr.at[j]).start())

    def own_wait(j0, j1):
        for j in range(j0, j1):
            if j < 2:
                pltpu.make_async_copy(res.at[3, :, pl.ds(width + j * HD, HD)], kv_all.at[kvrow(cp, z), pl.ds(j * HD, HD)], orr.at[j]).wait()
            elif j < nkv:
                pltpu.make_async_copy(res.at[3, :, pl.ds((j - 2) * HD, HD)], q_loc.at[arow(z), pl.ds((j - 2) * HD, HD)], orr.at[j]).wait()
            else:
                o = (j - nkv) * HD
                pltpu.make_async_copy(resd.at[3, :, pl.ds(o, HD)], do_loc.at[arow(z), pl.ds(o, HD)], orr.at[j]).wait()

    def got(j0, j1):
        for j in range(j0, j1):
            for k in range(3):
                t = src[k]
                if j < 2:
                    a = kv_all.at[kvrow(cp, t), pl.ds(j * HD, HD)]
                elif j < nkv:
                    a = q_loc.at[arow(t), pl.ds((j - 2) * HD, HD)]
                else:
                    a = do_loc.at[arow(t), pl.ds((j - nkv) * HD, HD)]
                rc(a, a, rs.at[j, k], rr.at[t, j], dz(t)).wait_recv()

    py = (1 - y) * 2 + c
    ts = [z] + src
    kva = [kv_all.at[kvrow(cp, t), :] for t in ts]
    kvb = [kv_all.at[kvrow(py, t), :] for t in ts]
    kyc = [rc(a, a, kys.at[j], kyr.at[j], dy) for j, a in enumerate(kva)]
    kyg = [rc(a, a, kys.at[j], kyr.at[j], dy) for j, a in enumerate(kvb)]
    kcc = [rc(a, a, kcs.at[j, 0], kcr.at[j, 0], dc) for j, a in enumerate(kva)]
    kcf = [rc(a, a, kcs.at[j, 1], kcr.at[j, 1], dc) for j, a in enumerate(kvb)]

    def kv1(j):
        if j == 0:
            own_wait(0, 2)
        else:
            t = ts[j]
            for b in range(2):
                a = kv_all.at[kvrow(cp, t), pl.ds(b * HD, HD)]
                rc(a, a, rs.at[b, j - 1], rr.at[t, b], dz(t)).wait_recv()
        kyc[j].start()
        kcc[j].start()

    def kv2(j):
        kyg[j].wait_recv()
        kcf[j].start()

    per = piece // BQ
    n_units = per * (n_pieces + 1)
    load_q = pltpu.make_async_copy(q_loc, qv, fs.at[0])
    load_kv = pltpu.make_async_copy(kv_all, kvv, fs.at[1])

    def fwd_load():
        for j in range(4):
            kcc[j].wait_recv()
            kcf[j].wait_recv()
        load_kv.start()
        own_wait(2, nkv)
        got(2, nkv)
        load_q.start()
        load_kv.wait()
        for b in range(n_pieces):
            vt_ref[:, b * piece:(b + 1) * piece] = kvv[b * piece:(b + 1) * piece, HD:].T
        load_q.wait()

    def o_out(i):
        return pltpu.make_async_copy(ost.at[i % 2], o_loc.at[pl.ds(pl.multiple_of(i * BQ, BQ), BQ), :], fs.at[2 + i % 2])

    def fwd_unit(u):
        n0 = cp + 1
        n1 = n_pieces - cp
        early = u < per * n0
        v = u - per * n0
        i = jnp.where(early, u // n0, per + v // n1)
        j = jnp.where(early, u % n0, v % n1)
        diag = j == jnp.where(early, n0, n1) - 1
        start = pl.multiple_of(piece_row(j, piece, n_pieces), BQ)
        qrow = pl.ds(pl.multiple_of(i * BQ, BQ), BQ)

        @pl.when(j == 0)
        def _():
            m_ref[...] = jnp.full_like(m_ref, NEG)
            l_ref[...] = jnp.zeros_like(l_ref)
            acc_ref[...] = jnp.zeros_like(acc_ref)

        def tile(masked):
            k = kvv[pl.ds(start, piece), :HD]
            vt = vt_ref[:, pl.ds(start, piece)]
            if masked:
                kr = lax.broadcasted_iota(jnp.int32, (piece, BQ), 0)
                qr = lax.broadcasted_iota(jnp.int32, (piece, BQ), 1)
                keep = kr <= qr + (i % per) * BQ
            scores = [mm(k, qv[qrow, h * HD:(h + 1) * HD], NT) for h in range(nh)]
            for h in range(nh):
                s = scores[h] * (SCALE * LOG2E)
                if masked:
                    s = jnp.where(keep, s, NEG)
                m_old = m_ref[h:h + 1, :]
                m_new = jnp.maximum(m_old, jnp.max(s, axis=0, keepdims=True))
                p = jnp.exp2(s - m_new)
                a = jnp.exp2(m_old - m_new)
                m_ref[h:h + 1, :] = m_new
                l_ref[h:h + 1, :] = l_ref[h:h + 1, :] * a + jnp.sum(p, axis=0, keepdims=True)
                o = mm(vt, p.astype(jnp.bfloat16), NN)
                acc_ref[h * HD:(h + 1) * HD, :] = acc_ref[h * HD:(h + 1) * HD, :] * a + o

        @pl.when(jnp.logical_not(diag))
        def _():
            tile(False)

        @pl.when(diag)
        def _():
            tile(True)

            @pl.when(i >= 2)
            def _():
                o_out(i).wait()

            for h in range(nh):
                l = l_ref[h:h + 1, :]
                o = acc_ref[h * HD:(h + 1) * HD, :] / l
                ost[i % 2, :, h * HD:(h + 1) * HD] = o.T.astype(jnp.bfloat16)
                lse_ref[i, h:h + 1, :] = m_ref[h:h + 1, :] + jnp.log2(l)
            o_out(i).start()

    own_in(0, lambda q: q.start())
    own_in(1, lambda q: q.start())
    own_do(0)
    own_in(2, lambda q: q.start())
    own_do(1)

    f0 = 3 * nkv + FWD_AT
    f1 = n + 5

    def once(i, at, f, *args):
        pl.when(i == at)(functools.partial(f, *args))

    def step(i, _):
        stage(i, st1)
        stage(i - 1, st2)
        stage(i - 2, st3)
        stage(i - 3, st4)
        st6(i - 5)
        st5(i - 4)
        j = i // 3

        @pl.when(jnp.logical_and(i % 3 == 1, jnp.logical_and(j >= 2, j < nb)))
        def _():
            own_do(j)

        @pl.when(jnp.logical_and(i % 3 == 2, jnp.logical_and(j >= 2, j + 1 < nb)))
        def _():
            own_in(j + 1, lambda q: q.start())

        once(i, 2, kv1, 0)
        for k in range(1, 4):
            once(i, 9 + k, kv1, k)
        for k in range(4):
            once(i, 12 + k, kv2, k)
        once(i, 2 * nkv, own_send, nkv, nb)
        once(i, f0, fwd_load)

        @pl.when(i > f0)
        def _():
            lax.fori_loop(n_units * (i - 1 - f0) // (f1 - f0), n_units * (i - f0) // (f1 - f0), lambda u, _: (fwd_unit(u), 0)[1], 0)

        return 0

    lax.fori_loop(0, f1 + 1, step, 0)

    for i in range(2 * per - 2, 2 * per):
        o_out(i).wait()
    for q in prim:
        q.wait_send()

    @pl.when(inner)
    def _():
        for q in sec:
            q.wait_send()

    def drain(i, _):
        def f(d, even):
            @pl.when(inner)
            def _():
                d['zf'].wait_send()
            for q in ['x', 'y', 'fy' if even else 'fx', 0, 1, 2, 3]:
                d[q].wait_send()

        stage(i, f)
        j, k, s = unit(i)
        result(j, k, z, lambda a, b: rc(a, b, rs.at[j, k], rr.at[z, j], dz(s)).wait_send())
        return 0

    lax.fori_loop(0, n, drain, 0)
    own_wait(nkv, nb)
    got(nkv, nb)
    for j in range(4):
        kyc[j].wait_send()
        kcc[j].wait_send()
        kcf[j].wait_send()


FWD_AT = 9


def input_phase(x, dy, wq, wk, wv, wo, cp_size):
    rows, d = x.shape
    width = wq.shape[1]
    cols = width + 2 * HD
    nb = 2 * (width // HD) + 2
    n = 3 * nb
    seq = 4 * rows
    piece = seq // 2
    keys = seq * cp_size
    bf, f32 = jnp.bfloat16, jnp.float32
    dma = pltpu.SemaphoreType.DMA
    hbm = pl.BlockSpec(memory_space=pltpu.HBM)
    vmem = pl.BlockSpec(memory_space=pltpu.VMEM)
    sds = jax.ShapeDtypeStruct
    out_shape = [sds((4, d, cols), bf), sds((4, width, d), bf), sds((seq, width), bf), sds((keys, 2 * HD), bf),
                 sds((seq, width), bf), sds((seq, width), bf), sds((seq // BQ, 8, BQ), f32)]
    scratch = [pltpu.VMEM((2, d, HD), bf), pltpu.VMEM((2, HD, d), bf), pltpu.VMEM((2, d, HD), bf), pltpu.VMEM((2, HD, d), bf),
               pltpu.VMEM((4, rows, cols), bf), pltpu.VMEM((4, rows, width), bf), pltpu.VMEM((seq, width), bf),
               pltpu.VMEM((keys, 2 * HD), bf), pltpu.VMEM((HD, keys), bf), pltpu.VMEM((8, BQ), f32), pltpu.VMEM((8, BQ), f32),
               pltpu.VMEM((width, BQ), f32), pltpu.VMEM((2, BQ, width), bf),
               dma((5, nb)), dma((4, nb)), dma((n, 2)), dma((n, 2)), dma((n, 2)), dma((n, 2)), dma((n, 4)), dma((n, 4)),
               dma((2,)), dma((3,)), dma((nb,)), dma((nb, 3)), dma((4, nb)), dma((4,)), dma((4,)), dma((4, 2)), dma((4, 2)),
               dma((4,))]
    return pl.pallas_call(
        functools.partial(input_kernel, piece, keys // piece),
        out_shape=out_shape,
        in_specs=[vmem, vmem] + [hbm] * 4,
        out_specs=[hbm] * 6 + [vmem],
        scratch_shapes=scratch,
        name="input_phase",
        compiler_params=pltpu.CompilerParams(collective_id=1, has_side_effects=True, vmem_limit_bytes=VMEM),
        cost_estimate=pl.CostEstimate(flops=10 ** 11, bytes_accessed=10 ** 7, transcendentals=0))(x, dy, wq, wk, wv, wo)


def y_kernel(o_ref, w_ref, y_ref):
    acc = mm(o_ref[0], w_ref[0], NN)
    for g in range(1, o_ref.shape[0]):
        acc = acc + mm(o_ref[g], w_ref[g], NN)
    y_ref[...] = acc.astype(jnp.bfloat16)


def y_proj(o, wo):
    ng, rows, nq = o.shape
    d = wo.shape[2]
    bn = 512
    return pl.pallas_call(
        y_kernel, grid=(d // bn,),
        out_shape=jax.ShapeDtypeStruct((rows, d), jnp.bfloat16),
        in_specs=[pl.BlockSpec((ng, rows, nq), lambda j: (0, 0, 0)), pl.BlockSpec((ng, nq, bn), lambda j: (0, 0, j))],
        out_specs=pl.BlockSpec((rows, bn), lambda j: (0, j)),
        name="y_proj", compiler_params=pltpu.CompilerParams(vmem_limit_bytes=VMEM),
        cost_estimate=pl.CostEstimate(flops=2 * rows * d * nq * ng, bytes_accessed=30 * 10 ** 6, transcendentals=0))(o, wo)


def dx_kernel(dq_ref, dkv_ref, w_ref, dx_ref):
    nq = dq_ref.shape[2]
    acc = None
    for g in range(dq_ref.shape[0]):
        t = mm(dq_ref[g], w_ref[g, :, :nq], NT) + mm(dkv_ref[g], w_ref[g, :, nq:], NT)
        acc = t if acc is None else acc + t
    dx_ref[...] = acc.astype(jnp.bfloat16)


def dx_proj(dq, dkv, wqkv):
    ng, rows, nq = dq.shape
    _, d, cols = wqkv.shape
    bn = 512
    return pl.pallas_call(
        dx_kernel, grid=(d // bn,),
        out_shape=jax.ShapeDtypeStruct((rows, d), jnp.bfloat16),
        in_specs=[pl.BlockSpec((ng, rows, nq), lambda j: (0, 0, 0)), pl.BlockSpec((ng, rows, 2 * HD), lambda j: (0, 0, 0)),
                  pl.BlockSpec((ng, bn, cols), lambda j: (0, j, 0))],
        out_specs=pl.BlockSpec((rows, bn), lambda j: (0, j)),
        name="dx_proj", compiler_params=pltpu.CompilerParams(vmem_limit_bytes=VMEM),
        cost_estimate=pl.CostEstimate(flops=2 * rows * d * cols * ng, bytes_accessed=40 * 10 ** 6, transcendentals=0))(dq, dkv, wqkv)


def piece_row(j, piece, n_pieces):
    half = n_pieces // 2
    return jnp.where(j < half, j * 2 * piece, (n_pieces - 1 - j) * 2 * piece + piece)


def key_loop(n, piece, n_pieces, tile):
    per = piece // BQ
    full = n // per

    def whole(j, _):
        tile(pl.multiple_of(piece_row(j, piece, n_pieces), BQ), piece, False)
        return 0

    def part(j, _):
        tile(pl.multiple_of(piece_row(full, piece, n_pieces) + (j - full * per) * BQ, BQ), BQ, False)
        return 0

    lax.fori_loop(0, full, whole, 0)
    lax.fori_loop(full * per, n, part, 0)
    tile(pl.multiple_of(piece_row(full, piece, n_pieces) + (n - full * per) * BQ, BQ), BQ, True)


def keep_mask(size):
    r = lax.broadcasted_iota(jnp.int32, (size, BQ), 0)
    q = lax.broadcasted_iota(jnp.int32, (size, BQ), 1)
    return r <= q


def bwd_kernel(nh, piece, n_pieces, pos_ref, q_ref, do_ref, o_ref, lse_ref, kv_ref, dq_ref, dkv_ref, kt_ref, del_ref, dqt_ref):
    i = pl.program_id(0)
    n = pos_ref[i]

    @pl.when(i == 0)
    def _():
        dkv_ref[...] = jnp.zeros_like(dkv_ref)
        for b in range(n_pieces):
            kt_ref[:, b * piece:(b + 1) * piece] = kv_ref[b * piece:(b + 1) * piece, :HD].T

    for h in range(nh):
        sl = slice(h * HD, (h + 1) * HD)
        pr = do_ref[:, sl].astype(jnp.float32) * o_ref[:, sl].astype(jnp.float32)
        del_ref[h:h + 1, :] = jnp.sum(pr.T, axis=0, keepdims=True)
    dqt_ref[...] = jnp.zeros_like(dqt_ref)

    def tile(start, size, masked):
        for t0 in range(0, size, BQ):
            sub(start + t0, masked)

    def sub(start, masked):
        size = BQ
        k = kv_ref[pl.ds(start, size), :HD]
        v = kv_ref[pl.ds(start, size), HD:]
        kt = kt_ref[:, pl.ds(start, size)]
        dv = None
        dk = None
        for h in range(nh):
            sl = slice(h * HD, (h + 1) * HD)
            s = mm(k, q_ref[:, sl], NT) * (SCALE * LOG2E) - lse_ref[0, h:h + 1, :]
            dp = mm(v, do_ref[:, sl], NT)
            if masked:
                s = jnp.where(keep_mask(size), s, NEG)
            pb = jnp.exp2(s).astype(jnp.bfloat16)
            ds = (pb.astype(jnp.float32) * (dp - del_ref[h:h + 1, :])).astype(jnp.bfloat16)
            dvh = mm(pb, do_ref[:, sl], NN)
            dkh = mm(ds, q_ref[:, sl], NN)
            dv = dvh if dv is None else dv + dvh
            dk = dkh if dk is None else dk + dkh
            dqt_ref[sl, :] += mm(kt, ds, NN)
        dkv_ref[pl.ds(start, size), :HD] += dk * SCALE
        dkv_ref[pl.ds(start, size), HD:] += dv

    key_loop(n, piece, n_pieces, tile)
    for h in range(nh):
        sl = slice(h * HD, (h + 1) * HD)
        dq_ref[:, sl] = (dqt_ref[sl, :] * SCALE).T.astype(jnp.bfloat16)


def attn_bwd(pos, q, do, o, lse, kv, piece):
    rows, width = q.shape
    nh = width // HD
    keys = kv.shape[0]
    nq = rows // BQ
    row = pl.BlockSpec((BQ, width), lambda i, p: (i, 0))
    gs = pltpu.PrefetchScalarGridSpec(
        num_scalar_prefetch=1, grid=(nq,),
        in_specs=[row, row, row, pl.BlockSpec((1, 8, BQ), lambda i, p: (i, 0, 0)),
                  pl.BlockSpec((keys, 2 * HD), lambda i, p: (0, 0))],
        out_specs=[row, pl.BlockSpec((keys, 2 * HD), lambda i, p: (0, 0))],
        scratch_shapes=[pltpu.VMEM((HD, keys), jnp.bfloat16), pltpu.VMEM((8, BQ), jnp.float32),
                        pltpu.VMEM((width, BQ), jnp.float32)])
    return pl.pallas_call(
        functools.partial(bwd_kernel, nh, piece, keys // piece),
        out_shape=[jax.ShapeDtypeStruct(q.shape, jnp.bfloat16), jax.ShapeDtypeStruct((keys, 2 * HD), jnp.float32)],
        grid_spec=gs, name="attn_bwd", compiler_params=pltpu.CompilerParams(vmem_limit_bytes=VMEM),
        cost_estimate=pl.CostEstimate(flops=150 * 10 ** 9, bytes_accessed=10 ** 7, transcendentals=0))(pos, q, do, o, lse, kv)


def solution(mesh):
    cp_size = mesh.shape['cp']
    row_spec = P(('dp', 'cp', 'tp'), None)

    def local_step(x_blk, dy_blk, w_query, w_key, w_value, w_out):
        rows, d = x_blk.shape
        ng = mesh.shape['tp']
        seq_loc = rows * ng
        piece = seq_loc // 2
        width = w_query.shape[1]
        rank = lax.axis_index('cp')
        half = piece // BQ
        t = jnp.arange(2 * half, dtype=jnp.int32)
        pos = jnp.where(t < half, rank * half + t, (2 * cp_size - 1 - rank) * half + t - half).astype(jnp.int32)

        def a2a(v):
            return lax.all_to_all(v, 'tp', 0, 0, tiled=True)

        wqkv, wo, q_loc, kv_all, do_loc, o_loc, lse = input_phase(x_blk, dy_blk, w_query, w_key, w_value, w_out, cp_size)
        o_g = a2a(o_loc.reshape(ng, rows, width))
        dq_loc, dkv = attn_bwd(pos, q_loc, do_loc, o_loc, lse, kv_all, piece)
        y_blk = y_proj(o_g, wo)
        dq_g = a2a(dq_loc.reshape(ng, rows, width))
        dkv_own = lax.psum_scatter(dkv, 'cp', scatter_dimension=0, tiled=True).astype(jnp.bfloat16)
        dkv_g = a2a(dkv_own.reshape(ng, rows, 2 * HD))
        dx_blk = dx_proj(dq_g, dkv_g, wqkv)
        return y_blk, dx_blk

    return jax.shard_map(local_step, mesh=mesh, in_specs=(row_spec, row_spec, P(None, 'tp'), P(None, 'tp'), P(None, 'tp'), P('tp', None)),
                         out_specs=(row_spec, row_spec), check_vma=False)
```

time: 794 us -> 643 us (0.81)
  Pallas kernels: 596 us -> 492 us
  waiting for transfers between devices: 83.6 us -> 60.1 us
  starting transfers between devices: 19.3 us -> 7.2 us
    pallas_call x5 -> x1, Pallas kernels: 419 us -> 315 us  [input_phase(): pl.pallas_call(functools.partial(input_kernel, piece, keys // piece), out...]
    all_to_all x5 -> x2, waiting for transfers between devices: 82.9 us -> 60 us  [a2a(): return lax.all_to_all(v, 'tp', 0, 0, tiled=True)]
    all_to_all x5 -> x2, starting transfers between devices: 19 us -> 7.16 us  [a2a(): return lax.all_to_all(v, 'tp', 0, 0, tiled=True)]
  transfers between devices with their start and end apart: 7 -> 3, of which waited for: 4 -> 2; matrix products, arithmetic and copies ran while one was open for 0% -> 0% of each run, Pallas kernels for 35% -> 3%
where the time goes in v3:
time: 643 us; the launch traced here: 642 us
  Pallas kernels  492 us (77%)
  blocking collectives  62.6 us (10%)
  waiting for transfers between devices  60.1 us (9%)
  between operations  14.1 us (2%)
  starting transfers between devices  7.2 us (1%)
    pallas_call x1, Pallas kernels, input_phase(): pl.pallas_call(functools.partial(input_kernel, piece, keys // piece), out...  315 us
    pallas_call x1, Pallas kernels, attn_bwd(): pl.pallas_call(functools.partial(bwd_kernel, nh, piece, keys // piece), o...  139 us
    all_to_all x1, blocking collectives, a2a(): return lax.all_to_all(v, 'tp', 0, 0, tiled=True)  62.6 us
    all_to_all x2, waiting for transfers between devices, a2a(): return lax.all_to_all(v, 'tp', 0, 0, tiled=True)  60 us
    pallas_call x1, Pallas kernels, dx_proj(): pl.pallas_call(dx_kernel, grid=(d // bn,), out_shape=jax.ShapeDtypeStruct...  20.5 us
    pallas_call x1, Pallas kernels, y_proj(): pl.pallas_call(y_kernel, grid=(d // bn,), out_shape=jax.ShapeDtypeStruct(...  17.4 us
  transfers between devices with their start and end apart: 3, of which 2 were waited for; matrix products, arithmetic and copies ran while one was open for 0% of the time, Pallas kernels for 3%

profile of v3, /device:TPU:0, one launch (start us, length us, event | category | flops | bytes accessed | tf_op | source)
XLA Modules:
  0.0 641.5 jit_solution(9603428081727936370)
XLA Ops:
  7.2 0.0 reduce-scatter.2.cloned.1.call-start
  7.2 0.5 compare_select_fusion.pos_ref
  7.7 314.7 %input_phase.1 = (bf16[4,3584,1152]{2,1,0:T(8,128)(2,1)}, bf16[4,896,3584]{2,1,0:T(8,128)(2,1)}, bf16[1536,896]{1,0:T(8,128)(2,1)}, bf16[6144,256]{1,0:T(8,128)(...) custom-call(bf16[384,3584]{1,0:T(8,128)(2,1)} %x_ref.1, ...), custom_call_target="tpu_custom_call" | custom-call | flops 99999997952 | bytes 10000000 | tf_op jit(solution)/shard_map/input_phase/pallas_call | solution.py:481
  322.5 139.3 %attn_bwd.1 = (bf16[1536,896]{1,0:T(8,128)(2,1)}, f32[6144,256]{1,0:T(8,128)}) custom-call(s32[6]{0:T(128)} %compare_select_fusion.pos_ref, bf16[1536,896]{1,0:T(8,128)(2,1)} %get-tuple-element.13.q_ref, bf16[1536,896]{1,0:T(8,128)(2,1)} %get-tuple-element.14.do_ref, bf16[1536,896]{1,0:T(8,128)(2,1)} %get-tuple-element.11.o_ref, ...), custom_call_target="tpu_custom_call" | custom-call | flops 149999992832 | bytes 10000000 | tf_op jit(solution)/shard_map/attn_bwd/pallas_call | solution.py:625
  461.8 0.0 copy-start.1
  461.8 0.0 reduce-scatter.2.cloned.1.call-update
  461.8 1.8 copy-done.1
  463.6 62.6 %all_to_all.15.o_ref = bf16[4,384,896]{2,1,0:T(8,128)(2,1)} all-to-all(bf16[4,384,896]{2,1,0:T(8,128)(2,1)S(1)} %bitcast.4), channel_id=1, replica_groups=mesh['dp'=2,'tp'=4,'cp'=4] {'tp'}, dimensions={0} | all-to-all | bytes 5505024 | tf_op jit(solution)/shard_map/all_to_all | solution.py:648
  526.2 3.7 all-to-all-start.1
  529.9 0.0 reduce-scatter.2.cloned.1.call-done
  529.9 2.4 convert_element_type.3
  532.3 58.0 %all-to-all-done.1.dq_ref = bf16[4,384,896]{2,1,0:T(8,128)(2,1)S(1)} async-done(((bf16[4,384,896]{2,1,0:T(8,128)(2,1)}), bf16[4,384,896]{2,1,0:T(8,128)(2,1)S(1)}, u32[]{:S(2)}, u32[]{:S(2)}) %all-to-all-start.1) | async-done | bytes 2752544 | tf_op jit(solution)/shard_map/all_to_all | solution.py:648
  590.3 0.0 copy-start
  590.3 3.5 all-to-all-start.2
  593.8 17.4 %y_proj.1 = bf16[384,3584]{1,0:T(8,128)(2,1)} custom-call(bf16[4,384,896]{2,1,0:T(8,128)(2,1)} %all_to_all.15.o_ref, bf16[4,896,3584]{2,1,0:T(8,128)(2,1)} %get-tuple-element.12.w_ref), custom_call_target="tpu_custom_call" | custom-call | flops 9865003008 | bytes 30000000 | tf_op jit(solution)/shard_map/y_proj/pallas_call | solution.py:503
  611.3 0.0 copy-done
  611.3 2.0 all-to-all-done.2.dkv_ref
  613.3 0.0 copy-start.2
  613.3 0.9 copy-done.2
  614.2 20.5 %dx_proj.1 = bf16[384,3584]{1,0:T(8,128)(2,1)} custom-call(bf16[4,384,896]{2,1,0:T(8,128)(2,1)} %copy-done, bf16[4,384,256]{2,1,0:T(8,128)(2,1)} %copy-done.2, bf16[4,3584,1152]{2,1,0:T(8,128)(2,1)} %get-tuple-element.19.w_ref), custom_call_target="tpu_custom_call" | custom-call | flops 12683575296 | bytes 40000000 | tf_op jit(solution)/shard_map/dx_proj/pallas_call | solution.py:525
Async XLA Ops:
  7.2 522.7 %reduce-scatter.2.cloned.1.call-start = ((), (), s32[]{:S(2)}) async-start(), calls=%async_computation.4 | async-start | bytes 7864320 | tf_op jit(solution)/shard_map/reduce_scatter | solution.py:655
  461.8 1.8 copy-start.1
  526.2 64.1 %all-to-all-start.1 = ((bf16[4,384,896]{2,1,0:T(8,128)(2,1)}), bf16[4,384,896]{2,1,0:T(8,128)(2,1)S(1)}, u32[]{:S(2)}, u32[]{:S(2)}) async-start(bf16[4,384,896]{2,1,0:T(8,128)(2,1)} %bitcast.3), calls=%async_computation.1 | async-start | bytes 5505024 | tf_op jit(solution)/shard_map/all_to_all | solution.py:648
  590.3 21.0 %copy-start = (bf16[4,384,896]{2,1,0:T(8,128)(2,1)}, bf16[4,384,896]{2,1,0:T(8,128)(2,1)S(1)}, u32[]{:S(2)}) copy-start(bf16[4,384,896]{2,1,0:T(8,128)(2,1)S(1)} %all-to-all-done.1.dq_ref) | copy-start | bytes 8257540
  590.3 22.9 %all-to-all-start.2 = ((bf16[4,384,256]{2,1,0:T(8,128)(2,1)}), bf16[4,384,256]{2,1,0:T(8,128)(2,1)S(1)}, u32[]{:S(2)}, u32[]{:S(2)}) async-start(bf16[4,384,256]{2,1,0:T(8,128)(2,1)} %bitcast.2), calls=%async_computation.3 | async-start | bytes 1572864 | tf_op jit(solution)/shard_map/all_to_all | solution.py:648
  613.3 0.9 copy-start.2
Sparse Core Ops, SparseCore 0:
  461.9 56.5 reduce-scatter.1

commit v4 on v3

--- a/solution.py
+++ b/solution.py
@@ -489,69 +489,9 @@
         cost_estimate=pl.CostEstimate(flops=10 ** 11, bytes_accessed=10 ** 7, transcendentals=0))(x, dy, wq, wk, wv, wo)
 
 
-def y_kernel(o_ref, w_ref, y_ref):
-    acc = mm(o_ref[0], w_ref[0], NN)
-    for g in range(1, o_ref.shape[0]):
-        acc = acc + mm(o_ref[g], w_ref[g], NN)
-    y_ref[...] = acc.astype(jnp.bfloat16)
-
-
-def y_proj(o, wo):
-    ng, rows, nq = o.shape
-    d = wo.shape[2]
-    bn = 512
-    return pl.pallas_call(
-        y_kernel, grid=(d // bn,),
-        out_shape=jax.ShapeDtypeStruct((rows, d), jnp.bfloat16),
-        in_specs=[pl.BlockSpec((ng, rows, nq), lambda j: (0, 0, 0)), pl.BlockSpec((ng, nq, bn), lambda j: (0, 0, j))],
-        out_specs=pl.BlockSpec((rows, bn), lambda j: (0, j)),
-        name="y_proj", compiler_params=pltpu.CompilerParams(vmem_limit_bytes=VMEM),
-        cost_estimate=pl.CostEstimate(flops=2 * rows * d * nq * ng, bytes_accessed=30 * 10 ** 6, transcendentals=0))(o, wo)
-
-
-def dx_kernel(dq_ref, dkv_ref, w_ref, dx_ref):
-    nq = dq_ref.shape[2]
-    acc = None
-    for g in range(dq_ref.shape[0]):
-        t = mm(dq_ref[g], w_ref[g, :, :nq], NT) + mm(dkv_ref[g], w_ref[g, :, nq:], NT)
-        acc = t if acc is None else acc + t
-    dx_ref[...] = acc.astype(jnp.bfloat16)
-
-
-def dx_proj(dq, dkv, wqkv):
-    ng, rows, nq = dq.shape
-    _, d, cols = wqkv.shape
-    bn = 512
-    return pl.pallas_call(
-        dx_kernel, grid=(d // bn,),
-        out_shape=jax.ShapeDtypeStruct((rows, d), jnp.bfloat16),
-        in_specs=[pl.BlockSpec((ng, rows, nq), lambda j: (0, 0, 0)), pl.BlockSpec((ng, rows, 2 * HD), lambda j: (0, 0, 0)),
-                  pl.BlockSpec((ng, bn, cols), lambda j: (0, j, 0))],
-        out_specs=pl.BlockSpec((rows, bn), lambda j: (0, j)),
-        name="dx_proj", compiler_params=pltpu.CompilerParams(vmem_limit_bytes=VMEM),
-        cost_estimate=pl.CostEstimate(flops=2 * rows * d * cols * ng, bytes_accessed=40 * 10 ** 6, transcendentals=0))(dq, dkv, wqkv)
-
-
 def piece_row(j, piece, n_pieces):
     half = n_pieces // 2
     return jnp.where(j < half, j * 2 * piece, (n_pieces - 1 - j) * 2 * piece + piece)
-
-
-def key_loop(n, piece, n_pieces, tile):
-    per = piece // BQ
-    full = n // per
-
-    def whole(j, _):
-        tile(pl.multiple_of(piece_row(j, piece, n_pieces), BQ), piece, False)
-        return 0
-
-    def part(j, _):
-        tile(pl.multiple_of(piece_row(full, piece, n_pieces) + (j - full * per) * BQ, BQ), BQ, False)
-        return 0
-
-    lax.fori_loop(0, full, whole, 0)
-    lax.fori_loop(full * per, n, part, 0)
-    tile(pl.multiple_of(piece_row(full, piece, n_pieces) + (n - full * per) * BQ, BQ), BQ, True)
 
 
 def keep_mask(size):
@@ -560,73 +500,286 @@
     return r <= q
 
 
-def bwd_kernel(nh, piece, n_pieces, pos_ref, q_ref, do_ref, o_ref, lse_ref, kv_ref, dq_ref, dkv_ref, kt_ref, del_ref, dqt_ref):
-    i = pl.program_id(0)
-    n = pos_ref[i]
-
-    @pl.when(i == 0)
-    def _():
-        dkv_ref[...] = jnp.zeros_like(dkv_ref)
-        for b in range(n_pieces):
-            kt_ref[:, b * piece:(b + 1) * piece] = kv_ref[b * piece:(b + 1) * piece, :HD].T
-
-    for h in range(nh):
-        sl = slice(h * HD, (h + 1) * HD)
-        pr = do_ref[:, sl].astype(jnp.float32) * o_ref[:, sl].astype(jnp.float32)
-        del_ref[h:h + 1, :] = jnp.sum(pr.T, axis=0, keepdims=True)
-    dqt_ref[...] = jnp.zeros_like(dqt_ref)
-
-    def tile(start, size, masked):
-        for t0 in range(0, size, BQ):
-            sub(start + t0, masked)
-
-    def sub(start, masked):
-        size = BQ
-        k = kv_ref[pl.ds(start, size), :HD]
-        v = kv_ref[pl.ds(start, size), HD:]
-        kt = kt_ref[:, pl.ds(start, size)]
-        dv = None
-        dk = None
+def output_kernel(piece, n_pieces, q_ref, do_ref, o_ref, lse_ref, kv_ref, wqkv, wo, y_ref, dx_ref,
+                  kt_ref, del_ref, dqt_ref, dkv_ref, stg, og, dqg, dkg, cbuf, ybuf, fin, wob, wqb, wkb, acc, tile_out,
+                  os, orr, qs, qr, cs, cr, ys, yr, ks, kr, ls, ts):
+    width = q_ref.shape[1]
+    nh = width // HD
+    rows = og.shape[1]
+    d = wo.shape[2]
+    x = lax.axis_index('dp')
+    z = lax.axis_index('tp')
+    cp = lax.axis_index('cp')
+    y = cp // 2
+    c = cp % 2
+    hz = z // 2
+    src = [1 - z + 4 * hz, 2 - hz, 3 - 3 * hz]
+    dy = (x, z, (1 - y) * 2 + c)
+    dc = (x, z, y * 2 + 1 - c)
+
+    def dz(s):
+        return (x, s, cp)
+
+    def rc(a, b, ss, rsem, dev):
+        return pltpu.make_async_remote_copy(src_ref=a, dst_ref=b, send_sem=ss, recv_sem=rsem, device_id=dev,
+                                            device_id_type=MESH_ID)
+
+    bar = pltpu.get_barrier_semaphore()
+    for dev in [dz(src[0]), dz(src[1]), dz(src[2]), dy, dc]:
+        pl.semaphore_signal(bar, inc=1, device_id=dev, device_id_type=MESH_ID)
+    pl.semaphore_wait(bar, 5)
+
+    def arow(t):
+        return pl.ds(pl.multiple_of(t * rows, 16), rows)
+
+    osend = [rc(o_ref.at[arow(t), :], og.at[z], os.at[k], orr.at[z], dz(t)) for k, t in enumerate(src)]
+    orecv = [rc(o_ref.at[arow(t), :], og.at[t], os.at[k], orr.at[t], dz(t)) for k, t in enumerate(src)]
+    for q in osend:
+        q.start()
+    og[z] = o_ref[arow(z), :]
+
+    per = piece // BQ
+    half = BQ // 2
+    dkv_ref[...] = jnp.zeros_like(dkv_ref)
+    for b in range(n_pieces):
+        kt_ref[:, b * piece:(b + 1) * piece] = kv_ref[b * piece:(b + 1) * piece, :HD].T
+
+    def dq_send(i, u, f):
+        r0 = i * BQ + u * half
+        t = r0 // rows
+        r = pl.multiple_of(r0 - t * rows, half)
+
+        @pl.when(t != z)
+        def _():
+            f(rc(stg.at[i % 2, pl.ds(u * half, half), :], dqg.at[z, pl.ds(r, half), :], qs.at[i % 2, u],
+                 qr.at[z, r // half], dz(t)))
+
+    def query_tile(ii, _):
+        i = (ii + per) % (2 * per)
+        n = jnp.where(i < per, cp * per + i, (n_pieces - 1 - cp) * per + i - per)
+        qrow = pl.ds(pl.multiple_of(i * BQ, BQ), BQ)
         for h in range(nh):
             sl = slice(h * HD, (h + 1) * HD)
-            s = mm(k, q_ref[:, sl], NT) * (SCALE * LOG2E) - lse_ref[0, h:h + 1, :]
-            dp = mm(v, do_ref[:, sl], NT)
-            if masked:
-                s = jnp.where(keep_mask(size), s, NEG)
-            pb = jnp.exp2(s).astype(jnp.bfloat16)
-            ds = (pb.astype(jnp.float32) * (dp - del_ref[h:h + 1, :])).astype(jnp.bfloat16)
-            dvh = mm(pb, do_ref[:, sl], NN)
-            dkh = mm(ds, q_ref[:, sl], NN)
-            dv = dvh if dv is None else dv + dvh
-            dk = dkh if dk is None else dk + dkh
-            dqt_ref[sl, :] += mm(kt, ds, NN)
-        dkv_ref[pl.ds(start, size), :HD] += dk * SCALE
-        dkv_ref[pl.ds(start, size), HD:] += dv
-
-    key_loop(n, piece, n_pieces, tile)
-    for h in range(nh):
-        sl = slice(h * HD, (h + 1) * HD)
-        dq_ref[:, sl] = (dqt_ref[sl, :] * SCALE).T.astype(jnp.bfloat16)
-
-
-def attn_bwd(pos, q, do, o, lse, kv, piece):
-    rows, width = q.shape
-    nh = width // HD
+            pr = do_ref[qrow, sl].astype(jnp.float32) * o_ref[qrow, sl].astype(jnp.float32)
+            del_ref[h:h + 1, :] = jnp.sum(pr.T, axis=0, keepdims=True)
+        dqt_ref[...] = jnp.zeros_like(dqt_ref)
+
+        def sub(start, masked):
+            krow = pl.ds(start, BQ)
+            k = kv_ref[krow, :HD]
+            v = kv_ref[krow, HD:]
+            kt = kt_ref[:, krow]
+            dv = None
+            dk = None
+            for h in range(nh):
+                sl = slice(h * HD, (h + 1) * HD)
+                q = q_ref[qrow, sl]
+                do = do_ref[qrow, sl]
+                s = mm(k, q, NT) * (SCALE * LOG2E) - lse_ref[i, h:h + 1, :]
+                dp = mm(v, do, NT)
+                if masked:
+                    s = jnp.where(keep_mask(BQ), s, NEG)
+                pb = jnp.exp2(s).astype(jnp.bfloat16)
+                ds = (pb.astype(jnp.float32) * (dp - del_ref[h:h + 1, :])).astype(jnp.bfloat16)
+                dvh = mm(pb, do, NN)
+                dkh = mm(ds, q, NN)
+                dv = dvh if dv is None else dv + dvh
+                dk = dkh if dk is None else dk + dkh
+                dqt_ref[sl, :] += mm(kt, ds, NN)
+            dkv_ref[krow, :HD] += dk
+            dkv_ref[krow, HD:] += dv
+
+        full = n // per
+
+        def whole(j, _):
+            start = piece_row(j, piece, n_pieces)
+            for t0 in range(0, piece, BQ):
+                sub(pl.multiple_of(start + t0, BQ), False)
+            return 0
+
+        def part(j, _):
+            sub(pl.multiple_of(piece_row(full, piece, n_pieces) + (j - full * per) * BQ, BQ), False)
+            return 0
+
+        lax.fori_loop(0, full, whole, 0)
+        lax.fori_loop(full * per, n, part, 0)
+        sub(pl.multiple_of(piece_row(full, piece, n_pieces) + (n - full * per) * BQ, BQ), True)
+
+        @pl.when(ii >= 2)
+        def _():
+            for u in range(2):
+                dq_send((ii - 2 + per) % (2 * per), u, lambda q: q.wait_send())
+
+        for h in range(nh):
+            sl = slice(h * HD, (h + 1) * HD)
+            stg[i % 2, :, sl] = (dqt_ref[sl, :] * SCALE).T.astype(jnp.bfloat16)
+        for u in range(2):
+            dq_send(i, u, lambda q: q.start())
+            r0 = i * BQ + u * half
+            t = r0 // rows
+
+            @pl.when(t == z)
+            def _(u=u, r0=r0, t=t):
+                dqg[z, pl.ds(pl.multiple_of(r0 - t * rows, half), half), :] = stg[i % 2, u * half:(u + 1) * half, :]
+
+        return 0
+
+    lax.fori_loop(0, 2 * per, query_tile, 0)
+
+    seq = 2 * piece
+
+    def kvblock(b):
+        return pl.ds(pl.multiple_of(b * seq, BQ), seq)
+
+    csend = [rc(dkv_ref.at[kvblock(2 * yy + 1 - c), :], cbuf.at[q], cs.at[q], cr.at[q], dc) for q, yy in enumerate((1 - y, y))]
+    for q in csend:
+        q.start()
+
+    bn = wob.shape[3]
+    nt = d // bn
+
+    def load_o(j):
+        return pltpu.make_async_copy(wo.at[:, :, pl.ds(pl.multiple_of(j * bn, bn), bn)], wob.at[j % 2], ls.at[j % 2])
+
+    def load_q(j):
+        return pltpu.make_async_copy(wqkv.at[:, pl.ds(pl.multiple_of(j * bn, bn), bn), pl.ds(0, width)], wqb.at[j % 2], ls.at[2 + j % 2])
+
+    def load_kv(j):
+        return pltpu.make_async_copy(wqkv.at[:, pl.ds(pl.multiple_of(j * bn, bn), bn), pl.ds(width, 2 * HD)], wkb.at[j % 2], ls.at[4 + j % 2])
+
+    def store(ref, j):
+        return pltpu.make_async_copy(tile_out.at[j % 2], ref.at[:, pl.ds(pl.multiple_of(j * bn, bn), bn)], ts.at[j % 2])
+
+    load_o(0).start()
+    load_o(1).start()
+    csend[0].wait_recv()
+    other = kvblock(2 * (1 - y) + c)
+    dkv_ref[other, :] += cbuf[0]
+    ysend = rc(dkv_ref.at[other, :], ybuf, ys, yr, dy)
+    ysend.start()
+    for q in orecv:
+        q.wait_recv()
+
+    def y_tile(j, _):
+        load_o(j).wait()
+        t = mm(og[0], wob[j % 2, 0], NN)
+        for g in range(1, 4):
+            t = t + mm(og[g], wob[j % 2, g], NN)
+
+        @pl.when(j >= 2)
+        def _():
+            store(y_ref, j - 2).wait()
+
+        tile_out[j % 2] = t.astype(jnp.bfloat16)
+        store(y_ref, j).start()
+
+        @pl.when(j + 2 < nt)
+        def _():
+            load_o(j + 2).start()
+
+        return 0
+
+    load_q(0).start()
+    load_q(1).start()
+    lax.fori_loop(0, nt, y_tile, 0)
+    for j in range(nt - 2, nt):
+        store(y_ref, j).wait()
+
+    for k in range(3):
+        for u in range(rows // half):
+            a = dqg.at[src[k], pl.ds(u * half, half), :]
+            rc(a, a, qs.at[0, 0], qr.at[src[k], u], dz(src[k])).wait_recv()
+
+    def dxq_tile(j, _):
+        load_q(j).wait()
+        t = mm(dqg[0], wqb[j % 2, 0], NT)
+        for g in range(1, 4):
+            t = t + mm(dqg[g], wqb[j % 2, g], NT)
+        acc[j] = t
+
+        @pl.when(j + 2 < nt)
+        def _():
+            load_q(j + 2).start()
+
+        return 0
+
+    h0 = nt // 2
+    lax.fori_loop(0, h0, dxq_tile, 0)
+
+    csend[1].wait_recv()
+    ysend.wait_recv()
+    mine = kvblock(2 * y + c)
+    tot = dkv_ref[mine, :] + cbuf[1] + ybuf[...]
+    fin[:, :HD] = (tot[:, :HD] * SCALE).astype(jnp.bfloat16)
+    fin[:, HD:] = tot[:, HD:].astype(jnp.bfloat16)
+    ksend = [rc(fin.at[arow(t), :], dkg.at[z], ks.at[k], kr.at[z], dz(t)) for k, t in enumerate(src)]
+    krecv = [rc(fin.at[arow(t), :], dkg.at[t], ks.at[k], kr.at[t], dz(t)) for k, t in enumerate(src)]
+    for q in ksend:
+        q.start()
+    dkg[z] = fin[arow(z), :]
+    load_kv(0).start()
+    load_kv(1).start()
+    lax.fori_loop(h0, nt, dxq_tile, 0)
+    for q in krecv:
+        q.wait_recv()
+
+    def dx_tile(j, _):
+        load_kv(j).wait()
+        t = acc[j]
+        for g in range(4):
+            t = t + mm(dkg[g], wkb[j % 2, g], NT)
+
+        @pl.when(j >= 2)
+        def _():
+            store(dx_ref, j - 2).wait()
+
+        tile_out[j % 2] = t.astype(jnp.bfloat16)
+        store(dx_ref, j).start()
+
+        @pl.when(j + 2 < nt)
+        def _():
+            load_kv(j + 2).start()
+
+        return 0
+
+    lax.fori_loop(0, nt, dx_tile, 0)
+    for j in range(nt - 2, nt):
+        store(dx_ref, j).wait()
+    for q in osend + csend + ksend + [ysend]:
+        q.wait_send()
+    for ii in range(2 * per - 2, 2 * per):
+        for u in range(2):
+            dq_send((ii + per) % (2 * per), u, lambda q: q.wait_send())
+
+
+def output_phase(q, do, o, lse, kv, wqkv, wo):
+    seq, width = q.shape
     keys = kv.shape[0]
-    nq = rows // BQ
-    row = pl.BlockSpec((BQ, width), lambda i, p: (i, 0))
-    gs = pltpu.PrefetchScalarGridSpec(
-        num_scalar_prefetch=1, grid=(nq,),
-        in_specs=[row, row, row, pl.BlockSpec((1, 8, BQ), lambda i, p: (i, 0, 0)),
-                  pl.BlockSpec((keys, 2 * HD), lambda i, p: (0, 0))],
-        out_specs=[row, pl.BlockSpec((keys, 2 * HD), lambda i, p: (0, 0))],
-        scratch_shapes=[pltpu.VMEM((HD, keys), jnp.bfloat16), pltpu.VMEM((8, BQ), jnp.float32),
-                        pltpu.VMEM((width, BQ), jnp.float32)])
+    rows = seq // 4
+    piece = seq // 2
+    d = wo.shape[2]
+    bn = 256
+    nt = d // bn
+    bf, f32 = jnp.bfloat16, jnp.float32
+    dma = pltpu.SemaphoreType.DMA
+    hbm = pl.BlockSpec(memory_space=pltpu.HBM)
+    vmem = pl.BlockSpec(memory_space=pltpu.VMEM)
+    v = pltpu.VMEM
+    scratch = [v((HD, keys), bf), v((8, BQ), f32), v((width, BQ), f32), v((keys, 2 * HD), f32), v((2, BQ, width), bf),
+               v((4, rows, width), bf), v((4, rows, width), bf), v((4, rows, 2 * HD), bf), v((2, seq, 2 * HD), f32),
+               v((seq, 2 * HD), f32), v((seq, 2 * HD), bf), v((2, 4, width, bn), bf), v((2, 4, bn, width), bf),
+               v((2, 4, bn, 2 * HD), bf), v((nt, rows, bn), f32), v((2, rows, bn), bf),
+               dma((3,)), dma((4,)), dma((2, 2)), dma((4, 3)), dma((2,)), dma((2,)), dma, dma, dma((3,)), dma((4,)),
+               dma((6,)), dma((2,))]
     return pl.pallas_call(
-        functools.partial(bwd_kernel, nh, piece, keys // piece),
-        out_shape=[jax.ShapeDtypeStruct(q.shape, jnp.bfloat16), jax.ShapeDtypeStruct((keys, 2 * HD), jnp.float32)],
-        grid_spec=gs, name="attn_bwd", compiler_params=pltpu.CompilerParams(vmem_limit_bytes=VMEM),
-        cost_estimate=pl.CostEstimate(flops=150 * 10 ** 9, bytes_accessed=10 ** 7, transcendentals=0))(pos, q, do, o, lse, kv)
+        functools.partial(output_kernel, piece, keys // piece),
+        out_shape=[jax.ShapeDtypeStruct((rows, d), bf)] * 2,
+        in_specs=[vmem] * 5 + [hbm] * 2,
+        out_specs=[hbm] * 2,
+        scratch_shapes=scratch,
+        name="output_phase",
+        compiler_params=pltpu.CompilerParams(collective_id=2, has_side_effects=True, vmem_limit_bytes=VMEM),
+        cost_estimate=pl.CostEstimate(flops=10 ** 11, bytes_accessed=10 ** 7, transcendentals=0))(q, do, o, lse, kv, wqkv, wo)
 
 
 def solution(mesh):
@@ -634,28 +787,8 @@
     row_spec = P(('dp', 'cp', 'tp'), None)
 
     def local_step(x_blk, dy_blk, w_query, w_key, w_value, w_out):
-        rows, d = x_blk.shape
-        ng = mesh.shape['tp']
-        seq_loc = rows * ng
-        piece = seq_loc // 2
-        width = w_query.shape[1]
-        rank = lax.axis_index('cp')
-        half = piece // BQ
-        t = jnp.arange(2 * half, dtype=jnp.int32)
-        pos = jnp.where(t < half, rank * half + t, (2 * cp_size - 1 - rank) * half + t - half).astype(jnp.int32)
-
-        def a2a(v):
-            return lax.all_to_all(v, 'tp', 0, 0, tiled=True)
-
-        wqkv, wo, q_loc, kv_all, do_loc, o_loc, lse = input_phase(x_blk, dy_blk, w_query, w_key, w_value, w_out, cp_size)
-        o_g = a2a(o_loc.reshape(ng, rows, width))
-        dq_loc, dkv = attn_bwd(pos, q_loc, do_loc, o_loc, lse, kv_all, piece)
-        y_blk = y_proj(o_g, wo)
-        dq_g = a2a(dq_loc.reshape(ng, rows, width))
-        dkv_own = lax.psum_scatter(dkv, 'cp', scatter_dimension=0, tiled=True).astype(jnp.bfloat16)
-        dkv_g = a2a(dkv_own.reshape(ng, rows, 2 * HD))
-        dx_blk = dx_proj(dq_g, dkv_g, wqkv)
-        return y_blk, dx_blk
+        wqkv, wo, q, kv, do, o, lse = input_phase(x_blk, dy_blk, w_query, w_key, w_value, w_out, cp_size)
+        return tuple(output_phase(q, do, o, lse, kv, wqkv, wo))
 
     return jax.shard_map(local_step, mesh=mesh, in_specs=(row_spec, row_spec, P(None, 'tp'), P(None, 'tp'), P(None, 'tp'), P('tp', None)),
                          out_specs=(row_spec, row_spec), check_vma=False)

time: 643 us -> 540 us (0.84)
  blocking collectives: 62.6 us -> 0 us
  waiting for transfers between devices: 60.1 us -> 0 us
  Pallas kernels: 492 us -> 529 us
  between operations: 14.1 us -> 0.66 us
  starting transfers between devices: 7.2 us -> 0 us
    all_to_all x1 -> x0, blocking collectives: 62.6 us -> none  [a2a(): return lax.all_to_all(v, 'tp', 0, 0, tiled=True)]
    all_to_all x2 -> x0, waiting for transfers between devices: 60 us -> none  [a2a(): return lax.all_to_all(v, 'tp', 0, 0, tiled=True)]
    pallas_call x3 -> x1, Pallas kernels: 177 us -> 214 us  [output_phase(): pl.pallas_call(functools.partial(output_kernel, piece, keys // piece), ou...]
    all_to_all x2 -> x0, starting transfers between devices: 7.16 us -> none  [a2a(): return lax.all_to_all(v, 'tp', 0, 0, tiled=True)]
  transfers between devices with their start and end apart: 3 -> 0, of which waited for: 2 -> 0; matrix products, arithmetic and copies ran while one was open for 0% -> 0% of each run, Pallas kernels for 3% -> 0%
where the time goes in v4:
time: 540 us; the launch traced here: 534 us
  Pallas kernels  529 us (98%)
    pallas_call x1, Pallas kernels, input_phase(): pl.pallas_call(functools.partial(input_kernel, piece, keys // piece), out...  315 us
    pallas_call x1, Pallas kernels, output_phase(): pl.pallas_call(functools.partial(output_kernel, piece, keys // piece), ou...  214 us

profile of v4, /device:TPU:0, one launch (start us, length us, event | category | flops | bytes accessed | tf_op | source)
XLA Modules:
  0.0 534.4 jit_solution(6000120894260368557)
XLA Ops:
  0.6 314.7 %input_phase.1 = (bf16[4,3584,1152]{2,1,0:T(8,128)(2,1)}, bf16[4,896,3584]{2,1,0:T(8,128)(2,1)}, bf16[1536,896]{1,0:T(8,128)(2,1)}, bf16[6144,256]{1,0:T(8,128)(...) custom-call(bf16[384,3584]{1,0:T(8,128)(2,1)} %x_ref.1, ...), custom_call_target="tpu_custom_call" | custom-call | flops 99999997952 | bytes 10000000 | tf_op jit(solution)/shard_map/input_phase/pallas_call | solution.py:481
  315.3 213.8 %output_phase.1 = (bf16[384,3584]{1,0:T(8,128)(2,1)}, bf16[384,3584]{1,0:T(8,128)(2,1)}) custom-call(bf16[1536,896]{1,0:T(8,128)(2,1)} %get-tuple-element.9.q_ref, bf16[1536,896]{1,0:T(8,128)(2,1)} %get-tuple-element.10.do_ref, bf16[1536,896]{1,0:T(8,128)(2,1)} %get-tuple-element.11.o_ref, f32[6,8,256]{2,1,0:T(8,128)} %get-tuple-element.12.lse_ref, ...), custom_call_target="tpu_custom_call" | custom-call | flops 99999997952 | bytes 10000000 | tf_op jit(solution)/shard_map/output_phase/pallas_call | solution.py:774
  529.2 0.0 copy-start
  529.2 3.6 copy.10
  532.8 0.0 copy-done
  532.9 1.5 copy.11
Async XLA Ops:
  529.2 3.7 copy-start

commit v5 on v4

--- a/solution.py
+++ b/solution.py
@@ -344,12 +344,12 @@
                 keep = kr <= qr + (i % per) * BQ
             scores = [mm(k, qv[qrow, h * HD:(h + 1) * HD], NT) for h in range(nh)]
             for h in range(nh):
-                s = scores[h] * (SCALE * LOG2E)
+                s = scores[h]
                 if masked:
                     s = jnp.where(keep, s, NEG)
                 m_old = m_ref[h:h + 1, :]
-                m_new = jnp.maximum(m_old, jnp.max(s, axis=0, keepdims=True))
-                p = jnp.exp2(s - m_new)
+                m_new = jnp.maximum(m_old, jnp.max(s, axis=0, keepdims=True) * (SCALE * LOG2E))
+                p = jnp.exp2(s * (SCALE * LOG2E) - m_new)
                 a = jnp.exp2(m_old - m_new)
                 m_ref[h:h + 1, :] = m_new
                 l_ref[h:h + 1, :] = l_ref[h:h + 1, :] * a + jnp.sum(p, axis=0, keepdims=True)
@@ -452,7 +452,7 @@
         kcf[j].wait_send()
 
 
-FWD_AT = 9
+FWD_AT = 5
 
 
 def input_phase(x, dy, wq, wk, wv, wo, cp_size):
@@ -564,46 +564,55 @@
             del_ref[h:h + 1, :] = jnp.sum(pr.T, axis=0, keepdims=True)
         dqt_ref[...] = jnp.zeros_like(dqt_ref)
 
-        def sub(start, masked):
-            krow = pl.ds(start, BQ)
+        def sub(start, size, masked):
+            krow = pl.ds(start, size)
             k = kv_ref[krow, :HD]
             v = kv_ref[krow, HD:]
             kt = kt_ref[:, krow]
-            dv = None
-            dk = None
+
+            def front(h):
+                sl = slice(h * HD, (h + 1) * HD)
+                return mm(k, q_ref[qrow, sl], NT), mm(v, do_ref[qrow, sl], NT)
+
+            def back(h, pb, ds, dk, dv):
+                sl = slice(h * HD, (h + 1) * HD)
+                dvh = mm(pb, do_ref[qrow, sl], NN)
+                dkh = mm(ds, q_ref[qrow, sl], NN)
+                dqt_ref[sl, :] += mm(kt, ds, NN)
+                return (dkh, dvh) if dk is None else (dk + dkh, dv + dvh)
+
+            nxt = front(0)
+            prev = None
+            dk = dv = None
             for h in range(nh):
-                sl = slice(h * HD, (h + 1) * HD)
-                q = q_ref[qrow, sl]
-                do = do_ref[qrow, sl]
-                s = mm(k, q, NT) * (SCALE * LOG2E) - lse_ref[i, h:h + 1, :]
-                dp = mm(v, do, NT)
+                s, dp = nxt
+                if h + 1 < nh:
+                    nxt = front(h + 1)
+                if prev is not None:
+                    dk, dv = back(*prev, dk, dv)
+                s = s * (SCALE * LOG2E) - lse_ref[i, h:h + 1, :]
                 if masked:
-                    s = jnp.where(keep_mask(BQ), s, NEG)
+                    s = jnp.where(keep_mask(size), s, NEG)
                 pb = jnp.exp2(s).astype(jnp.bfloat16)
                 ds = (pb.astype(jnp.float32) * (dp - del_ref[h:h + 1, :])).astype(jnp.bfloat16)
-                dvh = mm(pb, do, NN)
-                dkh = mm(ds, q, NN)
-                dv = dvh if dv is None else dv + dvh
-                dk = dkh if dk is None else dk + dkh
-                dqt_ref[sl, :] += mm(kt, ds, NN)
+                prev = (h, pb, ds)
+            dk, dv = back(*prev, dk, dv)
             dkv_ref[krow, :HD] += dk
             dkv_ref[krow, HD:] += dv
 
         full = n // per
 
         def whole(j, _):
-            start = piece_row(j, piece, n_pieces)
-            for t0 in range(0, piece, BQ):
-                sub(pl.multiple_of(start + t0, BQ), False)
+            sub(pl.multiple_of(piece_row(j, piece, n_pieces), BQ), piece, False)
             return 0
 
         def part(j, _):
-            sub(pl.multiple_of(piece_row(full, piece, n_pieces) + (j - full * per) * BQ, BQ), False)
+            sub(pl.multiple_of(piece_row(full, piece, n_pieces) + (j - full * per) * BQ, BQ), BQ, False)
             return 0
 
         lax.fori_loop(0, full, whole, 0)
         lax.fori_loop(full * per, n, part, 0)
-        sub(pl.multiple_of(piece_row(full, piece, n_pieces) + (n - full * per) * BQ, BQ), True)
+        sub(pl.multiple_of(piece_row(full, piece, n_pieces) + (n - full * per) * BQ, BQ), BQ, True)
 
         @pl.when(ii >= 2)
         def _():

time: 540 us -> 512 us (0.948)
  Pallas kernels: 529 us -> 503 us
    pallas_call x1, Pallas kernels: 214 us -> 193 us  [output_phase(): pl.pallas_call(functools.partial(output_kernel, piece, keys // piece), ou...]
where the time goes in v5:
time: 512 us; the launch traced here: 509 us
  Pallas kernels  503 us (98%)
  local copies, waits for them, and re-layouts  5.18 us (1%)
    pallas_call x1, Pallas kernels, input_phase(): pl.pallas_call(functools.partial(input_kernel, piece, keys // piece), out...  309 us
    pallas_call x1, Pallas kernels, output_phase(): pl.pallas_call(functools.partial(output_kernel, piece, keys // piece), ou...  193 us

profile of v5, /device:TPU:0, one launch (start us, length us, event | category | flops | bytes accessed | tf_op | source)
XLA Modules:
  0.0 508.8 jit_solution(1492546595491893360)
XLA Ops:
  0.6 309.5 %input_phase.1 = (bf16[4,3584,1152]{2,1,0:T(8,128)(2,1)}, bf16[4,896,3584]{2,1,0:T(8,128)(2,1)}, bf16[1536,896]{1,0:T(8,128)(2,1)}, bf16[6144,256]{1,0:T(8,128)(...) custom-call(bf16[384,3584]{1,0:T(8,128)(2,1)} %x_ref.1, ...), custom_call_target="tpu_custom_call" | custom-call | flops 99999997952 | bytes 10000000 | tf_op jit(solution)/shard_map/input_phase/pallas_call | solution.py:481
  310.1 193.4 %output_phase.1 = (bf16[384,3584]{1,0:T(8,128)(2,1)}, bf16[384,3584]{1,0:T(8,128)(2,1)}) custom-call(bf16[1536,896]{1,0:T(8,128)(2,1)} %get-tuple-element.9.q_ref, bf16[1536,896]{1,0:T(8,128)(2,1)} %get-tuple-element.10.do_ref, bf16[1536,896]{1,0:T(8,128)(2,1)} %get-tuple-element.11.o_ref, f32[6,8,256]{2,1,0:T(8,128)} %get-tuple-element.12.lse_ref, ...), custom_call_target="tpu_custom_call" | custom-call | flops 99999997952 | bytes 10000000 | tf_op jit(solution)/shard_map/output_phase/pallas_call | solution.py:783
  503.6 0.0 copy-start
  503.6 3.6 copy.10
  507.2 0.0 copy-done
  507.2 1.5 copy.11
Async XLA Ops:
  503.6 3.7 copy-start
